TPU v7x, 128 devices: a whole 4x4x4 slice. The times are simulated.
128 devices in a mesh: shard: 32 (over z, y, core), width: 4 (over x).
Axes of the slice: x: 4, y: 4, z: 4, core: 2. Of those that a mesh axis runs over, the one named last changes fastest.
Arguments:
- weight_gate: float32 [2048, 8192], P('shard', 'width'), may hold values from -0.25 to 0.25
- moment_gate: float32 [2048, 8192], P('shard', 'width'), may hold values from -6 to 6
- square_gate: float32 [2048, 8192], P('shard', 'width'), may hold values from 0.1 to 10
- weight_up: float32 [2048, 8192], P('shard', 'width'), may hold values from -0.25 to 0.25
- moment_up: float32 [2048, 8192], P('shard', 'width'), may hold values from -6 to 6
- square_up: float32 [2048, 8192], P('shard', 'width'), may hold values from 0.1 to 10
- norm_train: float32 [2048], P(('shard', 'width')), may hold values from 0.25 to 1.75
- norm_step: float32 [2048], P(('shard', 'width')), may hold values from -0.3 to 0.3
Outputs:
- serving_gate: bfloat16 [2048, 8192], P(None, 'width')
- serving_up: bfloat16 [2048, 8192], P(None, 'width')
- scale_gate: float32 [8192], P('width')
- scale_up: float32 [8192], P('width')
- serve_norm: bfloat16 [2048], replicated
- whole_gate: float32 [2048, 8192], P('shard', 'width')
- whole_up: float32 [2048, 8192], P('shard', 'width')
All inputs are finite; a program needn't handle non-finite values. Where the computation divides by a largest or mean magnitude, that divisor is 1e-20 or more.
Results may differ from a plain program's by a relative error of at most 0.001.
Values may be sent and summed in bfloat16 or wider, within the bound.
A program may use at most 128 MiB of HBM per device.

v0:
```python
import jax
import jax.numpy as jnp
from jax import lax
from jax.sharding import Mesh
from jax.sharding import PartitionSpec as P

SHARD = ("shard_0", "shard_1", "shard_2")
SHARD_WIDTH = ("shard_0", "shard_1", "shard_2", "width")


learn_rate = 0.02
decay_rate = 0.1
tiny_value = 1e-08


def sent_to_all(x, axis):
    copies = jnp.broadcast_to(x, (lax.axis_size(axis), *x.shape))
    return lax.all_to_all(copies, axis, split_axis=0, concat_axis=0, tiled=True)


def of_everyone(x, axis):
    everything = sent_to_all(x, axis)
    return jnp.max(everything, axis=0)


def packed_total(arrays, axis):
    ends = [0]
    for a in arrays:
        ends.append(ends[-1] + a.size)
    total = of_everyone(jnp.concatenate([a.ravel() for a in arrays]), axis)
    return tuple((total[b:e].reshape(a.shape) for a, b, e in zip(arrays, ends, ends[1:])))


def in_one_piece(arrays, axis, dim, along):
    ends, at = ([], 0)
    for a in arrays[:-1]:
        at += a.shape[along]
        ends.append(at)
    both = jnp.concatenate(arrays, axis=along)
    return tuple(jnp.split(lax.all_gather(both, axis, axis=dim, tiled=True), ends, axis=along))


def laid_out(pieces, dim):
    pieces = jnp.moveaxis(pieces, 0, dim)
    lengths = pieces.shape
    return pieces.reshape(*lengths[:dim], lengths[dim] * lengths[dim + 1], *lengths[dim + 2 :])


def gather_in_order(x, axes, turns):
    pieces = x
    for k in turns:
        pieces = lax.all_gather(pieces, axes[k])
    done = turns[::-1]
    back = [done.index(k) for k in range(len(axes))]
    pieces = pieces.transpose(*back, *range(len(axes), pieces.ndim))
    return pieces.reshape(-1, *x.shape)


def gathered_by_axis(x, axes, turns, dim):
    return laid_out(gather_in_order(x, axes, turns), dim)


def body(
    weight_gate, moment_gate, square_gate, weight_up, moment_up, square_up, norm_train, norm_step
):
    whole_gate = weight_gate - learn_rate * (
        moment_gate / (jnp.sqrt(square_gate) + tiny_value) + decay_rate * weight_gate
    )
    whole_up = weight_up - learn_rate * (
        moment_up / (jnp.sqrt(square_up) + tiny_value) + decay_rate * weight_up
    )
    scale_gate, scale_up = packed_total(
        (jnp.max(jnp.abs(whole_gate), axis=0), jnp.max(jnp.abs(whole_up), axis=0)), SHARD
    )
    narrow_gate, narrow_up = (
        (whole_gate / scale_gate).astype(jnp.bfloat16),
        (whole_up / scale_up).astype(jnp.bfloat16),
    )
    serving_gate, serving_up = in_one_piece((narrow_gate, narrow_up), SHARD, 0, 1)
    serve_norm = gathered_by_axis(
        (norm_train + norm_step).astype(jnp.bfloat16), SHARD_WIDTH, (0, 1, 3, 2), 0
    )
    return (serving_gate, serving_up, scale_gate, scale_up, serve_norm, whole_gate, whole_up)


def solution(mesh):
    finer = Mesh(
        mesh.devices.reshape(4, 4, 2, mesh.shape["width"]),
        ("shard_0", "shard_1", "shard_2", "width"),
    )
    placed = (
        P(SHARD, "width"),
        P(SHARD, "width"),
        P(SHARD, "width"),
        P(SHARD, "width"),
        P(SHARD, "width"),
        P(SHARD, "width"),
        P(SHARD_WIDTH),
        P(SHARD_WIDTH),
    )
    return jax.shard_map(
        body,
        mesh=finer,
        in_specs=placed,
        out_specs=(
            P(None, "width"),
            P(None, "width"),
            P("width"),
            P("width"),
            P(),
            P(SHARD, "width"),
            P(SHARD, "width"),
        ),
        check_vma=False,
    )
```

profile of v0, /device:TPU:1, one launch (start us, length us, event | category | flops | bytes accessed | tf_op | source)
XLA Modules:
  0.0 121.8 jit_solution(3514926101087195006)
XLA Ops:
  7.2 0.0 copy-start.6
  7.2 0.0 copy-start.4
  7.2 0.0 copy-start.5
  7.2 0.0 all-gather.7.cloned.1.call-start
  7.2 2.4 %abs_reduce_fusion = (f32[2048]{0:T(1024)S(1)}, f32[64,2048]{1,0:T(8,128)S(1)}, f32[2048]{0:T(1024)S(1)}, f32[64,2048]{1,0:T(8,128)S(1)}) fusion(f32[64,2048]{1,0:T(8,128)} %param.11, f32[64,2048]{1,0:T(8,128)} %param.12, f32[64,2048]{1,0:T(8,128)} %param.13, f32[64,2048]{1,0:T(8,128)} %param.8, f32[64,2048]{1,0:T(8,128)} %param.9, f32[64,2048]{1,0:T(8,128)} %param.10), kind=kLoop, calls=%fused_computation.3 | loop fusion | flops 2093056 | bytes 4210688 | tf_op jit(solution)/shard_map/reduce_max | solution.py:73
  9.6 0.0 copy-start
  9.6 0.0 copy-start.1
  9.7 0.5 broadcast_in_dim.2
  10.1 20.8 %all_to_all.6 = f32[32,1,4096]{2,1,0:T(1,128)S(1)} all-to-all(f32[32,1,4096]{2,1,0:T(1,128)S(1)} %broadcast_in_dim.2), channel_id=1, replica_groups=mesh['shard_0'=4,'shard_1'=4,'shard_2'=2,'width'=4] {'shard_0','shard_1'..., dimensions={0} | all-to-all | bytes 1048576 | tf_op jit(solution)/shard_map/all_to_all | solution.py:18
  31.0 0.4 reduce_max.29
  31.3 0.0 copy-start.2
  31.3 0.0 copy-start.3
  31.5 0.8 pad_maximum_fusion
  32.3 0.0 all-gather.7.cloned.1.call-update
  32.3 0.0 copy-done.6
  32.3 0.6 dynamic-slice
  33.6 0.0 copy-done.4
  33.6 0.0 copy-done.5
  33.6 0.2 dynamic-update-slice
  33.8 6.8 %all-reduce = bf16[64]{0:T(256)(128)(2,1)S(1)} all-reduce(bf16[64]{0:T(256)(128)(2,1)S(1)} %dynamic-update-slice), channel_id=2, replica_groups=mesh['shard_0'=4,'shard_1'=4,'shard_2'=2,'width'=4] {'shard_0'}, use_global_device_ids=true, to_apply=%add | all-reduce | flops 64 | bytes 256
  40.7 0.1 reshape.27
  40.8 7.7 %all-gather.4 = bf16[4,4,16]{2,1,0:T(4,128)(2,1)S(1)} all-gather(bf16[1,4,16]{2,1,0:T(4,128)(2,1)S(1)} %reshape.27), channel_id=3, replica_groups=mesh['shard_0'=4,'shard_1'=4,'shard_2'=2,'width'=4] {'shard_1'}, dimensions={0}, use_global_device_ids=true | all-gather | bytes 640 | tf_op jit(solution)/shard_map/all_gather | solution.py:52
  48.5 9.8 %all-gather.2 = bf16[16,4,16]{2,1,0:T(4,128)(2,1)S(1)} all-gather(bf16[4,4,16]{2,1,0:T(4,128)(2,1)S(1)} %all-gather.4), channel_id=4, replica_groups=mesh['shard_0'=4,'shard_1'=4,'shard_2'=2,'width'=4] {'width'}, dimensions={0}, use_global_device_ids=true | all-gather | bytes 2560 | tf_op jit(solution)/shard_map/all_gather | solution.py:52
  58.4 6.4 %all-gather.3 = bf16[8,4,4,16]{3,2,1,0:T(4,128)(2,1)S(1)} all-gather(bf16[4,4,4,16]{3,2,1,0:T(4,128)(2,1)S(1)} %bitcast.8), channel_id=5, replica_groups=mesh['shard_0'=4,'shard_1'=4,'shard_2'=2,'width'=4] {'shard_2'}, dimensions={0}, use_global_device_ids=true | all-gather | bytes 6144 | tf_op jit(solution)/shard_map/all_gather | solution.py:52
  64.8 0.7 reshape_reshape.3
  65.5 37.5 %all-gather.7.cloned.1.call-done = bf16[2048,4096]{1,0:T(8,128)(2,1)} async-done(((bf16[64,4096]{1,0:T(8,128)(2,1)}), bf16[2048,4096]{1,0:T(8,128)(2,1)}) %all-gather.7.cloned.1.call-update) | async-done | bytes 16777232 | tf_op jit(solution)/shard_map/all_gather | solution.py:40
  103.0 11.9 %fusion = (bf16[2048,2048]{1,0:T(8,128)(2,1)}, bf16[2048,2048]{1,0:T(8,128)(2,1)}) fusion(bf16[2048,4096]{1,0:T(8,128)(2,1)} %all-gather.7.cloned.1.call-done), kind=kLoop, calls=%fused_computation.10 | loop fusion | bytes 33554432 | tf_op jit(solution)/shard_map/split | solution.py:40
  115.0 0.0 copy-done
  115.0 0.0 copy-done.1
  115.0 0.0 copy-done.2
  115.0 0.0 copy-done.3
  (7 shorter events, 0.1 us)
Async XLA Ops:
  7.2 25.1 %copy-start.6 = (u32[128]{0:T(128)S(1)}, u32[128]{0:T(128)}, u32[]{:S(2)}) copy-start(u32[128]{0:T(128)} %constant.12) | copy-start | bytes 1540
  7.2 26.4 %copy-start.4 = (f32[16]{0:T(128)S(1)}, f32[16]{0:T(128)}, u32[]{:S(2)}) copy-start(f32[16]{0:T(128)} %param.14) | copy-start | bytes 196
  7.2 26.4 %copy-start.5 = (f32[16]{0:T(128)S(1)}, f32[16]{0:T(128)}, u32[]{:S(2)}) copy-start(f32[16]{0:T(128)} %param.15) | copy-start | bytes 196
  7.2 95.8 %all-gather.7.cloned.1.call-start = ((), (), s32[]{:S(2)}) async-start(), calls=%async_computation.1 | async-start | bytes 17301504 | tf_op jit(solution)/shard_map/all_gather | solution.py:40
  9.6 105.3 %copy-start = (f32[64,2048]{1,0:T(8,128)}, f32[64,2048]{1,0:T(8,128)S(1)}, u32[]{:S(2)}) copy-start(f32[64,2048]{1,0:T(8,128)S(1)} %get-tuple-element.10) | copy-start | bytes 1572868
  9.6 105.3 %copy-start.1 = (f32[64,2048]{1,0:T(8,128)}, f32[64,2048]{1,0:T(8,128)S(1)}, u32[]{:S(2)}) copy-start(f32[64,2048]{1,0:T(8,128)S(1)} %get-tuple-element.16) | copy-start | bytes 1572868
  31.3 83.6 %copy-start.2 = (f32[2048]{0:T(1024)}, f32[2048]{0:T(1024)S(1)}, u32[]{:S(2)}) copy-start(f32[2048]{0:T(1024)S(1)} %get-tuple-element.13) | copy-start | bytes 24580
  31.3 83.6 %copy-start.3 = (f32[2048]{0:T(1024)}, f32[2048]{0:T(1024)S(1)}, u32[]{:S(2)}) copy-start(f32[2048]{0:T(1024)S(1)} %get-tuple-element.14) | copy-start | bytes 24580
Sparse Core Ops, SparseCore 0:
  32.4 70.5 all-gather.6
where the time goes:
time: 122 us
  blocking collectives  51.6 us (42%)
  waiting for transfers between devices  37.6 us (31%)
  between operations  14.9 us (12%)
  local copies, waits for them, and re-layouts  14.1 us (12%)
  other arithmetic  3.66 us (3%)
    all_gather x1, waiting for transfers between devices, in_one_piece(): lax.all_gather(both, axis, axis=dim, tiled=True)  37.5 us
    all_gather x3, blocking collectives, gather_in_order(): pieces = lax.all_gather(pieces, axes[k])  24 us
    all_to_all x1, blocking collectives, sent_to_all(): return lax.all_to_all(copies, axis, split_axis=0, concat_axis=0, tiled=True)  20.8 us
    split x1, local copies, waits for them, and re-layouts, in_one_piece(): jnp.split(lax.all_gather(both, axis, axis=dim, tiled=True), ends, axis=al...  11.9 us
    unnamed x1, blocking collectives  6.83 us
  transfers between devices with their start and end apart: 1, of which 1 were waited for; matrix products, arithmetic and copies ran while one was open for 1% of the time, Pallas kernels for 0%

commit v1 on v0

v1 whole, which is shorter than its diff:
```python
import heapq

import jax
import jax.numpy as jnp
from jax import lax
from jax.experimental import pallas as pl
from jax.experimental.pallas import tpu as pltpu
from jax.sharding import PartitionSpec as P

MESH = pl.DeviceIdType.MESH

learn_rate = 0.02
decay_rate = 0.1
tiny_value = 1e-08

SIDE = 4
CUTS = 2
LANES = 128


def axis_of(array, turn):
    return array if turn == 0 else 1 - array


def onward(array, first, second, cut):
    low = cut < CUTS // 2
    out = []
    if second == 0:
        if first == 0:
            out += [(0, 1), (0, -1)]
        elif first == -1 and low:
            out += [(0, 1)]
        elif first == 1 and not low:
            out += [(0, -1)]
        out += [(1, 1), (1, -1)]
    elif second == -1 and low:
        out += [(1, 1)]
    elif second == 1 and not low:
        out += [(1, -1)]
    return [(axis_of(array, turn), step, turn) for turn, step in out]


def moved(first, second, turn, step):
    def one(offset):
        return {0: -step, -step: 2}[offset]

    return (one(first), second) if turn == 0 else (first, one(second))


def arrivals():
    free = {}
    queue = []
    order = []
    span, delay = 1.0, 0.7

    def send(chunk, now):
        array, first, second, cut = chunk
        for axis, step, turn in onward(*chunk):
            done = max(free.get((axis, step), 0.0), now) + span
            free[axis, step] = done
            there = (array, *moved(first, second, turn, step), cut)
            heapq.heappush(queue, (done + delay, there))

    for turn in (0, 1):
        for position in range(CUTS):
            for array in (0, 1):
                for axis, step, its_turn in onward(array, 0, 0, 0):
                    if its_turn != turn:
                        continue
                    cut = position if step == 1 else CUTS - 1 - position
                    done = free.get((axis, step), 0.0) + span
                    free[axis, step] = done
                    there = (array, *moved(0, 0, turn, step), cut)
                    heapq.heappush(queue, (done + delay, there))
    while queue:
        now, chunk = heapq.heappop(queue)
        order.append((now, chunk))
        send(chunk, now)
    return order


def kernel(
    wg, mg, sg, wu, mu, su, norm_train, norm_step,
    serving_g, serving_u, scale_g, scale_u, serve_norm, whole_g, whole_u,
    w_in, m_in, s_in, whole, big_g, big_u, local_max, other_max, y_buf, z_buf, q_buf,
    norm_row, norm_x, in_sem, out_sem, small_send, small_recv, ring_send, ring_recv,
    core_send, core_recv,
):
    rows, columns = wg.shape
    part = rows // CUTS
    me, x = lax.axis_index("shard"), lax.axis_index("width")
    core = lax.rem(me, 2)
    y = lax.rem(lax.div(me, 2), SIDE)
    z = lax.div(me, 2 * SIDE)

    def device(dz=0, dy=0, flip=False):
        zz, yy = lax.rem(z + dz + SIDE, SIDE), lax.rem(y + dy + SIDE, SIDE)
        cc = 1 - core if flip else core
        return (zz * SIDE + yy) * 2 + cc

    def near(axis, step):
        return (device(dy=step) if axis == 0 else device(dz=step), x)

    partner = (device(flip=True), x)
    y_peers = [(device(dy=k), x) for k in (1, 3, 2)]
    z_peers = [(device(dz=k), x) for k in (1, 3, 2)]
    x_peers = [(me, lax.rem(x + k, 4)) for k in (1, 3, 2)]
    peers = [partner, *y_peers, *z_peers, *x_peers]

    inputs = ((wg, mg, sg), (wu, mu, su))
    loads = []
    for a in (0, 1):
        loads.append(
            [
                pltpu.make_async_copy(src, dst.at[a], in_sem.at[a, k])
                for k, (src, dst) in enumerate(zip(inputs[a], (w_in, m_in, s_in)))
            ]
        )
        for copy in loads[a]:
            copy.start()

    barrier = pltpu.get_barrier_semaphore()
    for peer in peers:
        pl.semaphore_signal(barrier, inc=1, device_id=peer, device_id_type=MESH)

    gain = norm_train[...] + norm_step[...]
    for k in range(8):
        norm_row[:, 16 * k : 16 * (k + 1)] = gain
    lane = lax.broadcasted_iota(jnp.int32, (1, LANES), 1)
    mine = lax.div(lane, 16) == core * 4 + x
    norm_x[0] = jnp.where(mine, norm_row[...], 0.0)

    whole_out = (whole_g, whole_u)
    stores = []
    for a in (0, 1):
        for copy in loads[a]:
            copy.wait()

        @pl.loop(0, columns // LANES)
        def _(j):
            at = pl.ds(pl.multiple_of(j * LANES, LANES), LANES)
            weight = w_in[a, :, at]
            new = weight - learn_rate * (
                m_in[a, :, at] / (jnp.sqrt(s_in[a, :, at]) + tiny_value) + decay_rate * weight
            )
            whole[a, :, at] = new
            local_max[a, :, at] = jnp.max(jnp.abs(new), axis=0, keepdims=True)

        stores.append(pltpu.make_async_copy(whole.at[a], whole_out[a], out_sem.at[2 + a]))
        stores[a].start()

    pl.semaphore_wait(barrier, len(peers))

    sent = []

    def send_small(src, dst, slot, peer):
        copy = pltpu.make_async_remote_copy(
            src_ref=src,
            dst_ref=dst,
            send_sem=small_send.at[slot],
            recv_sem=small_recv.at[slot],
            device_id=peer,
            device_id_type=MESH,
        )
        copy.start()
        sent.append(copy)
        return copy

    swap = send_small(local_max.at[1 - core], other_max, 0, partner)
    gains = [send_small(norm_x.at[0], norm_x.at[k + 1], 1 + k, p) for k, p in enumerate(x_peers)]
    swap.wait_recv()
    for copy in gains:
        copy.wait_recv()
    y_buf[y, :, 0:columns] = jnp.maximum(local_max[core], other_max[...])
    y_buf[y, :, columns:] = norm_x[0] + norm_x[1] + norm_x[2] + norm_x[3]
    copies = [send_small(y_buf.at[y], y_buf.at[y], 4 + k, p) for k, p in enumerate(y_peers)]
    for copy in copies:
        copy.wait_recv()
    z_buf[z, :, 0:columns] = jnp.maximum(
        jnp.maximum(y_buf[0, :, 0:columns], y_buf[1, :, 0:columns]),
        jnp.maximum(y_buf[2, :, 0:columns], y_buf[3, :, 0:columns]),
    )
    for k in range(SIDE):
        z_buf[z, :, columns + k * LANES : columns + (k + 1) * LANES] = y_buf[k, :, columns:]
    copies = [send_small(z_buf.at[z], z_buf.at[z], 7 + k, p) for k, p in enumerate(z_peers)]
    for copy in copies:
        copy.wait_recv()
    q_buf[core, :, 0:columns] = jnp.maximum(
        jnp.maximum(z_buf[0, :, 0:columns], z_buf[1, :, 0:columns]),
        jnp.maximum(z_buf[2, :, 0:columns], z_buf[3, :, 0:columns]),
    )
    group = SIDE * LANES
    for k in range(SIDE):
        q_buf[core, :, columns + k * group : columns + (k + 1) * group] = z_buf[k, :, columns:]
    send_small(q_buf.at[core], q_buf.at[core], 10, partner).wait_recv()

    big = (big_g, big_u)
    serving = (serving_g, serving_u)
    own = pl.multiple_of(me * rows, rows)
    for a in (0, 1):

        @pl.loop(0, columns // LANES)
        def _(j):
            at = pl.ds(pl.multiple_of(j * LANES, LANES), LANES)
            factor = 1.0 / q_buf[a, :, at]
            big[a][pl.ds(own, rows), at] = (whole[a, :, at] * factor).astype(jnp.bfloat16)

    names = {}

    def number(chunk):
        return names.setdefault(chunk, len(names))

    def place(chunk, flip=False):
        array, first, second, cut = chunk
        dy, dz = (first, second) if array == 0 else (second, first)
        start = device(dz=dz, dy=dy, flip=flip) * rows + cut * part
        return pl.ds(pl.multiple_of(start, part), part)

    def pass_on(chunk, axis, step, turn):
        array, first, second, cut = chunk
        there = (array, *moved(first, second, turn, step), cut)
        piece = big[array].at[place(chunk)]
        copy = pltpu.make_async_remote_copy(
            src_ref=piece,
            dst_ref=piece,
            send_sem=ring_send.at[number(there)],
            recv_sem=ring_recv.at[number(there)],
            device_id=near(axis, step),
            device_id_type=MESH,
        )
        copy.start()
        sent.append(copy)

    def arrived(chunk):
        piece = big[chunk[0]].at[place(chunk)]
        pltpu.make_async_copy(piece, piece, ring_recv.at[number(chunk)]).wait()

    crossed = []

    def keep(chunk):
        array = chunk[0]
        piece = big[array].at[place(chunk)]
        copy = pltpu.make_async_remote_copy(
            src_ref=piece,
            dst_ref=piece,
            send_sem=core_send.at[len(crossed)],
            recv_sem=core_recv.at[len(crossed)],
            device_id=partner,
            device_id_type=MESH,
        )
        copy.start()
        sent.append(copy)
        crossed.append(chunk)
        pltpu.make_async_copy(piece, serving[array].at[place(chunk)], out_sem.at[array]).start()

    taken = 0

    def take():
        chunk = crossed[taken]
        where = place(chunk, flip=True)
        piece = big[chunk[0]].at[where]
        pltpu.make_async_copy(piece, piece, core_recv.at[taken]).wait()
        pltpu.make_async_copy(piece, serving[chunk[0]].at[where], out_sem.at[chunk[0]]).start()

    for turn in (0, 1):
        for position in range(CUTS):
            for array in (0, 1):
                for axis, step, its_turn in onward(array, 0, 0, 0):
                    if its_turn == turn:
                        cut = position if step == 1 else CUTS - 1 - position
                        pass_on((array, 0, 0, cut), axis, step, turn)
    for cut in range(CUTS):
        for array in (0, 1):
            keep((array, 0, 0, cut))
    scale_g[...] = q_buf[0, :, 0:columns]
    scale_u[...] = q_buf[1, :, 0:columns]
    serve_norm[...] = (q_buf[0, :, columns:] + q_buf[1, :, columns:]).astype(jnp.bfloat16)
    times = [0.0] * len(crossed)
    for now, chunk in arrivals():
        while taken < len(crossed) and times[taken] + 1.0 <= now:
            take()
            taken += 1
        arrived(chunk)
        for axis, step, turn in onward(*chunk):
            pass_on(chunk, axis, step, turn)
        keep(chunk)
        times.append(now)
    while taken < len(crossed):
        take()
        taken += 1
    for copy in sent:
        copy.wait_send()
    for a in (0, 1):
        stores[a].wait()
        pltpu.make_async_copy(big[a], serving[a], out_sem.at[a]).wait()


def body(wg, mg, sg, wu, mu, su, norm_train, norm_step):
    rows, columns = wg.shape
    total = rows * lax.axis_size("shard")
    chunks = 2 * CUTS * (SIDE * SIDE - 1)
    f32, bf16 = jnp.float32, jnp.bfloat16
    hbm, vmem = pl.BlockSpec(memory_space=pl.ANY), pl.BlockSpec(memory_space=pltpu.VMEM)
    dma = pltpu.SemaphoreType.DMA
    outs = pl.pallas_call(
        kernel,
        out_shape=(
            jax.ShapeDtypeStruct((total, columns), bf16),
            jax.ShapeDtypeStruct((total, columns), bf16),
            jax.ShapeDtypeStruct((1, columns), f32),
            jax.ShapeDtypeStruct((1, columns), f32),
            jax.ShapeDtypeStruct((1, 2048), bf16),
            jax.ShapeDtypeStruct((rows, columns), f32),
            jax.ShapeDtypeStruct((rows, columns), f32),
        ),
        in_specs=[hbm] * 6 + [vmem] * 2,
        out_specs=(hbm, hbm, vmem, vmem, vmem, hbm, hbm),
        scratch_shapes=[
            pltpu.VMEM((2, rows, columns), f32),
            pltpu.VMEM((2, rows, columns), f32),
            pltpu.VMEM((2, rows, columns), f32),
            pltpu.VMEM((2, rows, columns), f32),
            pltpu.VMEM((total, columns), bf16),
            pltpu.VMEM((total, columns), bf16),
            pltpu.VMEM((2, 1, columns), f32),
            pltpu.VMEM((1, columns), f32),
            pltpu.VMEM((SIDE, 1, columns + LANES), f32),
            pltpu.VMEM((SIDE, 1, columns + SIDE * LANES), f32),
            pltpu.VMEM((2, 1, columns + SIDE * SIDE * LANES), f32),
            pltpu.VMEM((1, LANES), f32),
            pltpu.VMEM((SIDE, 1, LANES), f32),
            dma((2, 3)),
            dma((4,)),
            dma((11,)),
            dma((11,)),
            dma((chunks,)),
            dma((chunks,)),
            dma((chunks + 2 * CUTS,)),
            dma((chunks + 2 * CUTS,)),
        ],
        compiler_params=pltpu.CompilerParams(
            collective_id=0, has_side_effects=True, vmem_limit_bytes=63 * 1024 * 1024
        ),
    )(wg, mg, sg, wu, mu, su, norm_train.reshape(1, -1), norm_step.reshape(1, -1))
    serving_g, serving_u, scale_g, scale_u, norm, whole_g, whole_u = outs
    return (
        serving_g,
        serving_u,
        scale_g.reshape(-1),
        scale_u.reshape(-1),
        norm.reshape(-1),
        whole_g,
        whole_u,
    )


def solution(mesh):
    both = P("shard", "width")
    flat = P(("shard", "width"))
    wide = P(None, "width")
    return jax.shard_map(
        body,
        mesh=mesh,
        in_specs=(both,) * 6 + (flat, flat),
        out_specs=(wide, wide, P("width"), P("width"), P(), both, both),
        check_vma=False,
    )
```

time: 122 us -> 91.8 us (0.75)
  Pallas kernels: 0 us -> 69.8 us
  blocking collectives: 51.6 us -> 0 us
  waiting for transfers between devices: 37.6 us -> 0 us
  between operations: 14.9 us -> 0.65 us
  local copies, waits for them, and re-layouts: 14.1 us -> 19.8 us
  other arithmetic: 3.66 us -> 1.32 us
    pallas_call x0 -> x1, Pallas kernels: none -> 69.8 us  [body(): pl.pallas_call(kernel, out_shape=(jax.ShapeDtypeStruct((total, columns),...]
    all_gather x1 -> x0, waiting for transfers between devices: 37.5 us -> none  [in_one_piece(): lax.all_gather(both, axis, axis=dim, tiled=True)]
    all_gather x3 -> x0, blocking collectives: 24 us -> none  [gather_in_order(): pieces = lax.all_gather(pieces, axes[k])]
    all_to_all x1 -> x0, blocking collectives: 20.8 us -> none  [sent_to_all(): return lax.all_to_all(copies, axis, split_axis=0, concat_axis=0, tiled=True)]
    unnamed x18 -> x14, local copies, waits for them, and re-layouts: 0.96 us -> 19.8 us
    split x1 -> x0, local copies, waits for them, and re-layouts: 11.9 us -> none  [in_one_piece(): jnp.split(lax.all_gather(both, axis, axis=dim, tiled=True), ends, axis=al...]
    unnamed x1 -> x0, blocking collectives: 6.83 us -> none
    reduce_max x2 -> x0, other arithmetic: 2.73 us -> none  [the longest x1 2.38 us: body(): jnp.max(jnp.abs(whole_up), axis=0)]
  transfers between devices with their start and end apart: 1 -> 0, of which waited for: 1 -> 0; matrix products, arithmetic and copies ran while one was open for 1% -> 0% of each run, Pallas kernels for 0% -> 0%
where the time goes in v1:
time: 91.8 us; the launch traced here: 91.6 us
  Pallas kernels  69.8 us (76%)
  local copies, waits for them, and re-layouts  19.8 us (22%)
  other arithmetic  1.32 us (1%)
    pallas_call x1, Pallas kernels, body(): pl.pallas_call(kernel, out_shape=(jax.ShapeDtypeStruct((total, columns),...  69.8 us
    unnamed x14, local copies, waits for them, and re-layouts  19.8 us

profile of v1, /device:TPU:1, one launch (start us, length us, event | category | flops | bytes accessed | tf_op | source)
XLA Modules:
  0.0 91.6 jit_solution(2679145828259762374)
XLA Ops:
  0.6 69.8 %shard_map.135 = (bf16[2048,2048]{1,0:T(8,128)(2,1)}, bf16[2048,2048]{1,0:T(8,128)(2,1)}, f32[1,2048]{1,0:T(1,128)}, f32[1,2048]{1,0:T(1,128)}, bf16[1,2048]{1,0...) custom-call(f32[64,2048]{1,0:T(8,128)} %wg.1, f32[64,2048]{1,0:T(8,128)} %mg.1, f32[64,2048]{1,0:T(8,128)} %sg.1, ...), custom_call_target="tpu_custom_call" | custom-call | tf_op jit(solution)/shard_map/pallas_call | solution.py:305
  70.5 1.3 %reduce = bf16[2048]{0:T(1024)(128)(2,1)} reduce(bf16[1,2048]{1,0:T(2,128)(2,1)} %get-tuple-element.18, bf16[]{:T(256)} %constant.2), dimensions={0}, to_apply=%get-tuple-element.18.reduce_sub_computation | reduce | bytes 8194 | tf_op jit(solution)/shard_map/pallas_call | solution.py:305
  71.8 8.4 %copy.21 = bf16[2048,2048]{1,0:T(8,128)(2,1)} copy(bf16[2048,2048]{1,0:T(8,128)(2,1)} %get-tuple-element.28) | data formatting | bytes 16777216
  80.2 0.0 copy-start.3
  80.2 0.0 copy-start.2
  80.2 0.0 copy-start.1
  80.3 0.0 copy-start
  80.3 8.5 %copy.22 = bf16[2048,2048]{1,0:T(8,128)(2,1)} copy(bf16[2048,2048]{1,0:T(8,128)(2,1)} %get-tuple-element.29) | data formatting | bytes 16777216
  88.8 0.0 copy-done.3
  88.8 0.6 copy.23
  89.4 0.0 copy-done.2
  89.4 0.6 copy.24
  90.0 0.0 copy-done.1
  90.0 0.8 copy.25
  90.8 0.0 copy-done
  90.8 0.8 copy.26
Async XLA Ops:
  80.2 8.5 %copy-start.3 = (f32[1,2048]{1,0:T(1,128)S(1)}, f32[1,2048]{1,0:T(1,128)}, u32[]{:S(2)}) copy-start(f32[1,2048]{1,0:T(1,128)} %get-tuple-element.16) | copy-start | bytes 24580
  80.2 9.1 %copy-start.2 = (f32[1,2048]{1,0:T(1,128)S(1)}, f32[1,2048]{1,0:T(1,128)}, u32[]{:S(2)}) copy-start(f32[1,2048]{1,0:T(1,128)} %get-tuple-element.17) | copy-start | bytes 24580
  80.2 9.7 %copy-start.1 = (f32[64,2048]{1,0:T(8,128)S(1)}, f32[64,2048]{1,0:T(8,128)}, u32[]{:S(2)}) copy-start(f32[64,2048]{1,0:T(8,128)} %get-tuple-element.33) | copy-start | bytes 1572868
  80.3 10.5 %copy-start = (f32[64,2048]{1,0:T(8,128)S(1)}, f32[64,2048]{1,0:T(8,128)}, u32[]{:S(2)}) copy-start(f32[64,2048]{1,0:T(8,128)} %get-tuple-element.34) | copy-start | bytes 1572868

commit v2 on v1

--- a/solution.py
+++ b/solution.py
@@ -16,6 +16,7 @@
 SIDE = 4
 CUTS = 2
 LANES = 128
+PARTS = 8
 
 
 def axis_of(array, turn):
@@ -81,9 +82,9 @@
 
 def kernel(
     wg, mg, sg, wu, mu, su, norm_train, norm_step,
-    serving_g, serving_u, scale_g, scale_u, serve_norm, whole_g, whole_u,
-    w_in, m_in, s_in, whole, big_g, big_u, local_max, other_max, y_buf, z_buf, q_buf,
-    norm_row, norm_x, in_sem, out_sem, small_send, small_recv, ring_send, ring_recv,
+    big_g, big_u, whole, scales,
+    w_in, m_in, s_in, local_max, other_max, y_buf, z_buf,
+    norm_row, norm_x, norm_in, in_sem, small_send, small_recv, ring_send, ring_recv,
     core_send, core_recv,
 ):
     rows, columns = wg.shape
@@ -108,11 +109,17 @@
     peers = [partner, *y_peers, *z_peers, *x_peers]
 
     inputs = ((wg, mg, sg), (wu, mu, su))
+    norms = [
+        pltpu.make_async_copy(src, norm_in.at[k], in_sem.at[6 + k])
+        for k, src in enumerate((norm_train, norm_step))
+    ]
+    for copy in norms:
+        copy.start()
     loads = []
     for a in (0, 1):
         loads.append(
             [
-                pltpu.make_async_copy(src, dst.at[a], in_sem.at[a, k])
+                pltpu.make_async_copy(src, dst.at[a], in_sem.at[3 * a + k])
                 for k, (src, dst) in enumerate(zip(inputs[a], (w_in, m_in, s_in)))
             ]
         )
@@ -123,15 +130,15 @@
     for peer in peers:
         pl.semaphore_signal(barrier, inc=1, device_id=peer, device_id_type=MESH)
 
-    gain = norm_train[...] + norm_step[...]
+    for copy in norms:
+        copy.wait()
+    gain = norm_in[0] + norm_in[1]
     for k in range(8):
         norm_row[:, 16 * k : 16 * (k + 1)] = gain
     lane = lax.broadcasted_iota(jnp.int32, (1, LANES), 1)
     mine = lax.div(lane, 16) == core * 4 + x
     norm_x[0] = jnp.where(mine, norm_row[...], 0.0)
 
-    whole_out = (whole_g, whole_u)
-    stores = []
     for a in (0, 1):
         for copy in loads[a]:
             copy.wait()
@@ -145,9 +152,6 @@
             )
             whole[a, :, at] = new
             local_max[a, :, at] = jnp.max(jnp.abs(new), axis=0, keepdims=True)
-
-        stores.append(pltpu.make_async_copy(whole.at[a], whole_out[a], out_sem.at[2 + a]))
-        stores[a].start()
 
     pl.semaphore_wait(barrier, len(peers))
 
@@ -185,24 +189,23 @@
     copies = [send_small(z_buf.at[z], z_buf.at[z], 7 + k, p) for k, p in enumerate(z_peers)]
     for copy in copies:
         copy.wait_recv()
-    q_buf[core, :, 0:columns] = jnp.maximum(
+    scales[core, :, 0:columns] = jnp.maximum(
         jnp.maximum(z_buf[0, :, 0:columns], z_buf[1, :, 0:columns]),
         jnp.maximum(z_buf[2, :, 0:columns], z_buf[3, :, 0:columns]),
     )
     group = SIDE * LANES
     for k in range(SIDE):
-        q_buf[core, :, columns + k * group : columns + (k + 1) * group] = z_buf[k, :, columns:]
-    send_small(q_buf.at[core], q_buf.at[core], 10, partner).wait_recv()
+        scales[core, :, columns + k * group : columns + (k + 1) * group] = z_buf[k, :, columns:]
+    send_small(scales.at[core], scales.at[core], 10, partner).wait_recv()
 
     big = (big_g, big_u)
-    serving = (serving_g, serving_u)
     own = pl.multiple_of(me * rows, rows)
     for a in (0, 1):
 
         @pl.loop(0, columns // LANES)
         def _(j):
             at = pl.ds(pl.multiple_of(j * LANES, LANES), LANES)
-            factor = 1.0 / q_buf[a, :, at]
+            factor = 1.0 / scales[a, :, at]
             big[a][pl.ds(own, rows), at] = (whole[a, :, at] * factor).astype(jnp.bfloat16)
 
     names = {}
@@ -251,7 +254,6 @@
         copy.start()
         sent.append(copy)
         crossed.append(chunk)
-        pltpu.make_async_copy(piece, serving[array].at[place(chunk)], out_sem.at[array]).start()
 
     taken = 0
 
@@ -260,7 +262,6 @@
         where = place(chunk, flip=True)
         piece = big[chunk[0]].at[where]
         pltpu.make_async_copy(piece, piece, core_recv.at[taken]).wait()
-        pltpu.make_async_copy(piece, serving[chunk[0]].at[where], out_sem.at[chunk[0]]).start()
 
     for turn in (0, 1):
         for position in range(CUTS):
@@ -272,9 +273,6 @@
     for cut in range(CUTS):
         for array in (0, 1):
             keep((array, 0, 0, cut))
-    scale_g[...] = q_buf[0, :, 0:columns]
-    scale_u[...] = q_buf[1, :, 0:columns]
-    serve_norm[...] = (q_buf[0, :, columns:] + q_buf[1, :, columns:]).astype(jnp.bfloat16)
     times = [0.0] * len(crossed)
     for now, chunk in arrivals():
         while taken < len(crossed) and times[taken] + 1.0 <= now:
@@ -290,9 +288,30 @@
         taken += 1
     for copy in sent:
         copy.wait_send()
-    for a in (0, 1):
-        stores[a].wait()
-        pltpu.make_async_copy(big[a], serving[a], out_sem.at[a]).wait()
+
+
+def deliver(
+    big_g, big_u, whole, scales,
+    serving_g, serving_u, scale_g, scale_u, serve_norm, whole_g, whole_u, sem,
+):
+    columns = big_g.shape[1]
+    copies = []
+
+    def put(src, dst):
+        copies.append(pltpu.make_async_copy(src, dst, sem.at[len(copies)]))
+        copies[-1].start()
+
+    step = big_g.shape[0] // PARTS
+    for src, dst in ((big_g, serving_g), (big_u, serving_u)):
+        for k in range(PARTS):
+            put(src.at[pl.ds(k * step, step)], dst.at[pl.ds(k * step, step)])
+    put(whole.at[0], whole_g)
+    put(whole.at[1], whole_u)
+    scale_g[...] = scales[0, :, 0:columns]
+    scale_u[...] = scales[1, :, 0:columns]
+    serve_norm[...] = (scales[0, :, columns:] + scales[1, :, columns:]).astype(jnp.bfloat16).reshape(-1)
+    for copy in copies:
+        copy.wait()
 
 
 def body(wg, mg, sg, wu, mu, su, norm_train, norm_step):
@@ -300,55 +319,63 @@
     total = rows * lax.axis_size("shard")
     chunks = 2 * CUTS * (SIDE * SIDE - 1)
     f32, bf16 = jnp.float32, jnp.bfloat16
-    hbm, vmem = pl.BlockSpec(memory_space=pl.ANY), pl.BlockSpec(memory_space=pltpu.VMEM)
+    hbm, vmem = pl.BlockSpec(memory_space=pltpu.HBM), pl.BlockSpec(memory_space=pltpu.VMEM)
     dma = pltpu.SemaphoreType.DMA
-    outs = pl.pallas_call(
+    gathered = pl.pallas_call(
         kernel,
+        out_shape=(
+            pltpu.VMEM((total, columns), bf16),
+            pltpu.VMEM((total, columns), bf16),
+            pltpu.VMEM((2, rows, columns), f32),
+            pltpu.VMEM((2, 1, columns + SIDE * SIDE * LANES), f32),
+        ),
+        in_specs=[hbm] * 8,
+        out_specs=(vmem,) * 4,
+        scratch_shapes=[
+            pltpu.VMEM((2, rows, columns), f32),
+            pltpu.VMEM((2, rows, columns), f32),
+            pltpu.VMEM((2, rows, columns), f32),
+            pltpu.VMEM((2, 1, columns), f32),
+            pltpu.VMEM((1, columns), f32),
+            pltpu.VMEM((SIDE, 1, columns + LANES), f32),
+            pltpu.VMEM((SIDE, 1, columns + SIDE * LANES), f32),
+            pltpu.VMEM((1, LANES), f32),
+            pltpu.VMEM((SIDE, 1, LANES), f32),
+            pltpu.VMEM((2, 1, 16), f32),
+            dma((8,)),
+            dma((11,)),
+            dma((11,)),
+            dma((chunks,)),
+            dma((chunks,)),
+            dma((chunks + 4 * CUTS,)),
+            dma((chunks + 4 * CUTS,)),
+        ],
+        compiler_params=pltpu.CompilerParams(
+            collective_id=0, has_side_effects=True, vmem_limit_bytes=47 * 1024 * 1024 - 300 * 1024
+        ),
+    )(wg, mg, sg, wu, mu, su, norm_train.reshape(1, -1), norm_step.reshape(1, -1))
+    serving_g, serving_u, scale_g, scale_u, norm, whole_g, whole_u = pl.pallas_call(
+        deliver,
         out_shape=(
             jax.ShapeDtypeStruct((total, columns), bf16),
             jax.ShapeDtypeStruct((total, columns), bf16),
             jax.ShapeDtypeStruct((1, columns), f32),
             jax.ShapeDtypeStruct((1, columns), f32),
-            jax.ShapeDtypeStruct((1, 2048), bf16),
+            jax.ShapeDtypeStruct((total,), bf16),
             jax.ShapeDtypeStruct((rows, columns), f32),
             jax.ShapeDtypeStruct((rows, columns), f32),
         ),
-        in_specs=[hbm] * 6 + [vmem] * 2,
+        in_specs=[vmem] * 4,
         out_specs=(hbm, hbm, vmem, vmem, vmem, hbm, hbm),
-        scratch_shapes=[
-            pltpu.VMEM((2, rows, columns), f32),
-            pltpu.VMEM((2, rows, columns), f32),
-            pltpu.VMEM((2, rows, columns), f32),
-            pltpu.VMEM((2, rows, columns), f32),
-            pltpu.VMEM((total, columns), bf16),
-            pltpu.VMEM((total, columns), bf16),
-            pltpu.VMEM((2, 1, columns), f32),
-            pltpu.VMEM((1, columns), f32),
-            pltpu.VMEM((SIDE, 1, columns + LANES), f32),
-            pltpu.VMEM((SIDE, 1, columns + SIDE * LANES), f32),
-            pltpu.VMEM((2, 1, columns + SIDE * SIDE * LANES), f32),
-            pltpu.VMEM((1, LANES), f32),
-            pltpu.VMEM((SIDE, 1, LANES), f32),
-            dma((2, 3)),
-            dma((4,)),
-            dma((11,)),
-            dma((11,)),
-            dma((chunks,)),
-            dma((chunks,)),
-            dma((chunks + 2 * CUTS,)),
-            dma((chunks + 2 * CUTS,)),
-        ],
-        compiler_params=pltpu.CompilerParams(
-            collective_id=0, has_side_effects=True, vmem_limit_bytes=63 * 1024 * 1024
-        ),
-    )(wg, mg, sg, wu, mu, su, norm_train.reshape(1, -1), norm_step.reshape(1, -1))
-    serving_g, serving_u, scale_g, scale_u, norm, whole_g, whole_u = outs
+        scratch_shapes=[dma((2 * PARTS + 2,))],
+        compiler_params=pltpu.CompilerParams(vmem_limit_bytes=24 * 1024 * 1024),
+    )(*gathered)
     return (
         serving_g,
         serving_u,
         scale_g.reshape(-1),
         scale_u.reshape(-1),
-        norm.reshape(-1),
+        norm,
         whole_g,
         whole_u,
     )

time: 91.8 us -> 76 us (0.83)
  local copies, waits for them, and re-layouts: 19.8 us -> 0 us
  Pallas kernels: 69.8 us -> 75.2 us
  other arithmetic: 1.32 us -> 0 us
    unnamed x14 -> x0, local copies, waits for them, and re-layouts: 19.8 us -> none
    pallas_call x1 -> x2, Pallas kernels: 69.8 us -> 75.2 us  [the longest x1 68.3 us: body(): pl.pallas_call(kernel, out_shape=(pltpu.VMEM((total, columns), bf16), plt...]
    pallas_call x1 -> x0, other arithmetic: 1.32 us -> none  [body(): pl.pallas_call(kernel, out_shape=(jax.ShapeDtypeStruct((total, columns),...]
where the time goes in v2:
time: 76 us; the launch traced here: 75.9 us
  Pallas kernels  75.2 us (99%)
    pallas_call x1, Pallas kernels, body(): pl.pallas_call(kernel, out_shape=(pltpu.VMEM((total, columns), bf16), plt...  68.3 us
    pallas_call x1, Pallas kernels, body(): pl.pallas_call(deliver, out_shape=(jax.ShapeDtypeStruct((total, columns),...  6.88 us

profile of v2, /device:TPU:1, one launch (start us, length us, event | category | flops | bytes accessed | tf_op | source)
XLA Modules:
  0.0 75.9 jit_solution(9539314266077688260)
XLA Ops:
  0.6 68.3 %shard_map.135 = (bf16[2048,2048]{1,0:T(8,128)(2,1)S(1)}, bf16[2048,2048]{1,0:T(8,128)(2,1)S(1)}, f32[2,64,2048]{2,1,0:T(8,128)S(1)}, f32[2,1,4096]{2,1,0:T(1,128)S(1)}) custom-call(f32[64,2048]{1,0:T(8,128)} %wg.1, f32[64,2048]{1,0:T(8,128)} %mg.1, f32[64,2048]{1,0:T(8,128)} %sg.1, f32[64,2048]{1,0:T(8,128)} %wu.1, f32[64,2048]{1,0:T(8,128)} %mu.1, ...), custom_call_target="tpu_custom_call" | custom-call | tf_op jit(solution)/shard_map/pallas_call | solution.py:324
  69.0 6.9 %shard_map.136 = (bf16[2048,2048]{1,0:T(8,128)(2,1)}, bf16[2048,2048]{1,0:T(8,128)(2,1)}, f32[1,2048]{1,0:T(1,128)}, f32[1,2048]{1,0:T(1,128)}, bf16[2048]{0:T(1...) custom-call(bf16[2048,2048]{1,0:T(8,128)(2,1)S(1)} %get-tuple-element.18.big_g, ...), custom_call_target="tpu_custom_call" | custom-call | tf_op jit(solution)/shard_map/pallas_call | solution.py:357

commit v3 on v2

v3 whole, which is shorter than its diff:
```python
import heapq

import jax
import jax.numpy as jnp
from jax import lax
from jax.experimental import pallas as pl
from jax.experimental.pallas import tpu as pltpu
from jax.sharding import PartitionSpec as P

MESH = pl.DeviceIdType.MESH

learn_rate = 0.02
decay_rate = 0.1
tiny_value = 1e-08

SIDE = 4
CUTS = 2
LANES = 128
PARTS = 2


def axis_of(array, turn):
    return array if turn == 0 else 1 - array


def onward(array, first, second, cut):
    low = cut < CUTS // 2
    out = []
    if second == 0:
        if first == 0:
            out += [(0, 1), (0, -1)]
        elif first == -1 and low:
            out += [(0, 1)]
        elif first == 1 and not low:
            out += [(0, -1)]
        out += [(1, 1), (1, -1)]
    elif second == -1 and low:
        out += [(1, 1)]
    elif second == 1 and not low:
        out += [(1, -1)]
    return [(axis_of(array, turn), step, turn) for turn, step in out]


def moved(first, second, turn, step):
    def one(offset):
        return {0: -step, -step: 2}[offset]

    return (one(first), second) if turn == 0 else (first, one(second))


def early(array, step):
    return 0 if step == 1 else CUTS - 1


def starts():
    for turn in (0, 1):
        for position in range(CUTS):
            for array in (0, 1):
                for axis, step, its_turn in onward(array, 0, 0, 0):
                    cut = position if step == 1 else CUTS - 1 - position
                    if its_turn == turn and not (turn == 0 and cut == early(array, step)):
                        yield (array, 0, 0, cut), axis, step, turn


def arrivals():
    free = {}
    queue = []
    order = []
    span, delay = 1.0, 0.7

    def send(chunk, axis, step, turn, now):
        array, first, second, cut = chunk
        done = max(free.get((axis, step), 0.0), now) + span
        free[axis, step] = done
        heapq.heappush(queue, (done + delay, (array, *moved(first, second, turn, step), cut)))

    for chunk, axis, step, turn in starts():
        send(chunk, axis, step, turn, 0.0)
    for array in (0, 1):
        for step in (1, -1):
            heapq.heappush(queue, (0.0, (array, -step, 0, early(array, step))))
    while queue:
        now, chunk = heapq.heappop(queue)
        order.append((chunk, now == 0.0))
        for axis, step, turn in onward(*chunk):
            send(chunk, axis, step, turn, now)
    return order


def kernel(
    wg, mg, sg, wu, mu, su, norm_train, norm_step,
    big_g, big_u, whole, scales,
    w_in, m_in, s_in, local_max, y_buf, z_buf, ahead, norm_in, norm_row, norm_x, norm_y,
    in_sem, small_send, small_recv, ahead_send, ahead_recv, ring_send, ring_recv, core_sem,
):
    rows, columns = wg.shape
    part = rows // CUTS
    me, x = lax.axis_index("shard"), lax.axis_index("width")
    core = lax.rem(me, 2)
    y = lax.rem(lax.div(me, 2), SIDE)
    z = lax.div(me, 2 * SIDE)

    def device(dz=0, dy=0, flip=0):
        zz, yy = lax.rem(z + dz + SIDE, SIDE), lax.rem(y + dy + SIDE, SIDE)
        cc = 1 - core if flip else core
        return (zz * SIDE + yy) * 2 + cc

    def near(axis, step):
        return (device(dy=step) if axis == 0 else device(dz=step), x)

    partner = (device(flip=1), x)
    steps = [(k, flip) for k in (2, 1, 3) for flip in (0, 1)] + [(0, 1)]
    x_peers = [(me, lax.rem(x + k, SIDE)) for k in (1, 2, 3)]
    peers = (
        [(device(dy=k, flip=f), x) for k, f in steps]
        + [(device(dz=k, flip=f), x) for k, f in steps if k]
        + x_peers
    )

    inputs = ((wg, mg, sg), (wu, mu, su))
    loads = [
        [
            pltpu.make_async_copy(src, dst.at[a], in_sem.at[3 * a + k])
            for k, (src, dst) in enumerate(zip(inputs[a], (w_in, m_in, s_in)))
        ]
        for a in (0, 1)
    ]
    norms = [
        pltpu.make_async_copy(src, norm_in.at[k], in_sem.at[6 + k])
        for k, src in enumerate((norm_train, norm_step))
    ]
    for copy in loads[0] + loads[1] + norms:
        copy.start()

    barrier = pltpu.get_barrier_semaphore()
    for peer in peers:
        pl.semaphore_signal(barrier, inc=1, device_id=peer, device_id_type=MESH)

    for a in (0, 1):
        for copy in loads[a]:
            copy.wait()

        @pl.loop(0, columns // LANES)
        def _(j):
            at = pl.ds(pl.multiple_of(j * LANES, LANES), LANES)
            weight = w_in[a, :, at]
            new = weight - learn_rate * (
                m_in[a, :, at] / (jnp.sqrt(s_in[a, :, at]) + tiny_value) + decay_rate * weight
            )
            whole[a, :, at] = new
            local_max[a, :, at] = jnp.max(jnp.abs(new), axis=0, keepdims=True)

    for copy in norms:
        copy.wait()
    gain = norm_in[0] + norm_in[1]
    for k in range(8):
        norm_row[:, 16 * k : 16 * (k + 1)] = gain
    lane = lax.broadcasted_iota(jnp.int32, (1, LANES), 1)
    mine = lax.div(lane, 16) == core * SIDE + x
    norm_x[3] = jnp.where(mine, norm_row[...], 0.0)

    pl.semaphore_wait(barrier, len(peers))

    def send(src, dst, send_sem, recv_sem, peer):
        pltpu.make_async_remote_copy(
            src_ref=src,
            dst_ref=dst,
            send_sem=send_sem,
            recv_sem=recv_sem,
            device_id=peer,
            device_id_type=MESH,
        ).start()

    def small(stage, src, dst, peer):
        send(src, dst, small_send.at[stage], small_recv.at[stage], peer)

    def await_bytes(ref, sem):
        pltpu.make_async_copy(ref, ref, sem).wait()

    for k, flip in steps:
        a = 1 - core if flip else core
        small(0, local_max.at[a], y_buf.at[2 * ((SIDE - k) % SIDE) + flip - 1], (device(dy=k, flip=flip), x))

    def send_ahead(array, step, half):
        cut, slot = early(array, step), 2 * array + (step == -1)
        size = part // 2
        send(
            whole.at[array, pl.ds(cut * part + half * size, size)],
            ahead.at[slot, pl.ds(half * size, size)],
            ahead_send,
            ahead_recv.at[slot],
            near(array, step),
        )

    for step in (1, -1):
        send_ahead(1, step, 0)
    for half in (0, 1):
        for step in (1, -1):
            send_ahead(0, step, half)
    for k, peer in enumerate(x_peers):
        small(2, norm_x.at[3], norm_x.at[k], peer)
    await_bytes(y_buf, small_recv.at[0])
    best = local_max[core]
    for k in range(7):
        best = jnp.maximum(best, y_buf[k])
    await_bytes(norm_x.at[pl.ds(0, 3)], small_recv.at[2])
    here = SIDE * core + z
    z_buf[here, :, 0:columns] = best
    z_buf[here, :, columns:] = norm_x[0] + norm_x[1] + norm_x[2] + norm_x[3]
    for k, flip in steps:
        small(1, z_buf.at[here], z_buf.at[here], (device(dz=k, flip=flip), x))
    for step in (1, -1):
        send_ahead(1, step, 1)
    await_bytes(z_buf.at[pl.ds(0, 7)], small_recv.at[1])

    big = (big_g, big_u)
    own = pl.multiple_of(me * rows, rows)
    for a in (0, 1):
        first = SIDE * a

        @pl.loop(0, columns // LANES)
        def _(j):
            at = pl.ds(pl.multiple_of(j * LANES, LANES), LANES)
            best = jnp.maximum(
                jnp.maximum(z_buf[first, :, at], z_buf[first + 1, :, at]),
                jnp.maximum(z_buf[first + 2, :, at], z_buf[first + 3, :, at]),
            )
            scales[a, :, at] = best
            factor = 1.0 / best
            big[a][pl.ds(own, rows), at] = (whole[a, :, at] * factor).astype(jnp.bfloat16)

    for k in range(SIDE):
        norm_y[y, :, k * LANES : (k + 1) * LANES] = z_buf[k, :, columns:] + z_buf[SIDE + k, :, columns:]
    for k in (1, 2, 3):
        small(3, norm_y.at[y], norm_y.at[y], (device(dy=k), x))

    names = {}

    def number(chunk):
        return names.setdefault(chunk, len(names))

    def place(chunk):
        array, first, second, cut = chunk
        dy, dz = (first, second) if array == 0 else (second, first)
        start = device(dz=dz, dy=dy) * rows + cut * part
        return pl.ds(pl.multiple_of(start, part), part)

    def pass_on(chunk, axis, step, turn):
        array, first, second, cut = chunk
        there = (array, *moved(first, second, turn, step), cut)
        piece = big[array].at[place(chunk)]
        send(piece, piece, ring_send, ring_recv.at[number(there)], near(axis, step))

    def cross(chunk):
        piece = big[chunk[0]].at[place(chunk)]
        send(piece, piece, core_sem.at[0], core_sem.at[1], partner)

    for chunk, axis, step, turn in starts():
        pass_on(chunk, axis, step, turn)
    for array in (0, 1):
        for cut in range(CUTS):
            cross((array, 0, 0, cut))
    for chunk, came_early in arrivals():
        array, first, second, cut = chunk
        if came_early:
            slot = 2 * array + (first == 1)
            await_bytes(ahead.at[slot], ahead_recv.at[slot])
            where = place(chunk)

            @pl.loop(0, columns // LANES)
            def _(j):
                at = pl.ds(pl.multiple_of(j * LANES, LANES), LANES)
                factor = 1.0 / scales[array, :, at]
                big[array][where, at] = (ahead[slot, :, at] * factor).astype(jnp.bfloat16)

        else:
            await_bytes(big[array].at[place(chunk)], ring_recv.at[number(chunk)])
        for axis, step, turn in onward(*chunk):
            pass_on(chunk, axis, step, turn)
        cross(chunk)

    await_bytes(norm_y.at[pl.ds(0, 3)], small_recv.at[3])
    for k in range(SIDE):
        for i in range(SIDE):
            at = columns + (k * SIDE + i) * LANES
            scales[0, :, at : at + LANES] = norm_y[i, :, k * LANES : (k + 1) * LANES]
    await_bytes(y_buf, small_send.at[0])
    await_bytes(z_buf.at[pl.ds(0, 7)], small_send.at[1])
    await_bytes(norm_x.at[pl.ds(0, 3)], small_send.at[2])
    await_bytes(norm_y.at[pl.ds(0, 3)], small_send.at[3])
    await_bytes(whole, ahead_send)
    passed = 2 * CUTS * (SIDE * SIDE - 1) - 4
    await_bytes(big_g.at[pl.ds(0, passed * part)], ring_send)
    await_bytes(big_g, core_sem.at[0])
    await_bytes(big_u, core_sem.at[1])


def deliver(
    big_g, big_u, whole, scales,
    serving_g, serving_u, scale_g, scale_u, serve_norm, whole_g, whole_u, sem,
):
    columns = big_g.shape[1]
    copies = []

    def put(src, dst):
        copies.append(pltpu.make_async_copy(src, dst, sem.at[len(copies)]))
        copies[-1].start()

    step = big_g.shape[0] // PARTS
    for src, dst in ((big_g, serving_g), (big_u, serving_u)):
        for k in range(PARTS):
            put(src.at[pl.ds(k * step, step)], dst.at[pl.ds(k * step, step)])
    put(whole.at[0], whole_g)
    put(whole.at[1], whole_u)
    scale_g[...] = scales[0, :, 0:columns]
    scale_u[...] = scales[1, :, 0:columns]
    serve_norm[...] = scales[0, :, columns:].astype(jnp.bfloat16).reshape(-1)
    for copy in copies:
        copy.wait()


def body(wg, mg, sg, wu, mu, su, norm_train, norm_step):
    rows, columns = wg.shape
    total = rows * lax.axis_size("shard")
    chunks = 2 * CUTS * (SIDE * SIDE - 1) - 4
    f32, bf16 = jnp.float32, jnp.bfloat16
    hbm, vmem = pl.BlockSpec(memory_space=pltpu.HBM), pl.BlockSpec(memory_space=pltpu.VMEM)
    dma = pltpu.SemaphoreType.DMA
    gathered = pl.pallas_call(
        kernel,
        out_shape=(
            pltpu.VMEM((total, columns), bf16),
            pltpu.VMEM((total, columns), bf16),
            pltpu.VMEM((2, rows, columns), f32),
            pltpu.VMEM((2, 1, columns + SIDE * SIDE * LANES), f32),
        ),
        in_specs=[hbm] * 8,
        out_specs=(vmem,) * 4,
        scratch_shapes=[
            pltpu.VMEM((2, rows, columns), f32),
            pltpu.VMEM((2, rows, columns), f32),
            pltpu.VMEM((2, rows, columns), f32),
            pltpu.VMEM((2, 1, columns), f32),
            pltpu.VMEM((7, 1, columns), f32),
            pltpu.VMEM((2 * SIDE, 1, columns + LANES), f32),
            pltpu.VMEM((4, rows // CUTS, columns), f32),
            pltpu.VMEM((2, 1, 16), f32),
            pltpu.VMEM((1, LANES), f32),
            pltpu.VMEM((SIDE, 1, LANES), f32),
            pltpu.VMEM((SIDE, 1, SIDE * LANES), f32),
            dma((8,)),
            dma((4,)),
            dma((4,)),
            dma,
            dma((4,)),
            dma,
            dma((chunks,)),
            dma((2,)),
        ],
        compiler_params=pltpu.CompilerParams(
            collective_id=0, has_side_effects=True, vmem_limit_bytes=47 * 1024 * 1024 - 300 * 1024
        ),
    )(wg, mg, sg, wu, mu, su, norm_train.reshape(1, -1), norm_step.reshape(1, -1))
    serving_g, serving_u, scale_g, scale_u, norm, whole_g, whole_u = pl.pallas_call(
        deliver,
        out_shape=(
            jax.ShapeDtypeStruct((total, columns), bf16),
            jax.ShapeDtypeStruct((total, columns), bf16),
            jax.ShapeDtypeStruct((1, columns), f32),
            jax.ShapeDtypeStruct((1, columns), f32),
            jax.ShapeDtypeStruct((total,), bf16),
            jax.ShapeDtypeStruct((rows, columns), f32),
            jax.ShapeDtypeStruct((rows, columns), f32),
        ),
        in_specs=[vmem] * 4,
        out_specs=(hbm, hbm, vmem, vmem, vmem, hbm, hbm),
        scratch_shapes=[dma((2 * PARTS + 2,))],
        compiler_params=pltpu.CompilerParams(vmem_limit_bytes=24 * 1024 * 1024),
    )(*gathered)
    return (
        serving_g,
        serving_u,
        scale_g.reshape(-1),
        scale_u.reshape(-1),
        norm,
        whole_g,
        whole_u,
    )


def solution(mesh):
    both = P("shard", "width")
    flat = P(("shard", "width"))
    wide = P(None, "width")
    return jax.shard_map(
        body,
        mesh=mesh,
        in_specs=(both,) * 6 + (flat, flat),
        out_specs=(wide, wide, P("width"), P("width"), P(), both, both),
        check_vma=False,
    )
```

time: 76 us -> 67.7 us (0.89)
  Pallas kernels: 75.2 us -> 67 us
    pallas_call x1, Pallas kernels: 68.3 us -> 60.2 us  [body(): pl.pallas_call(kernel, out_shape=(pltpu.VMEM((total, columns), bf16), plt...]
where the time goes in v3:
time: 67.7 us; the launch traced here: 67.6 us
  Pallas kernels  67 us (99%)
    pallas_call x1, Pallas kernels, body(): pl.pallas_call(kernel, out_shape=(pltpu.VMEM((total, columns), bf16), plt...  60.2 us
    pallas_call x1, Pallas kernels, body(): pl.pallas_call(deliver, out_shape=(jax.ShapeDtypeStruct((total, columns),...  6.77 us

profile of v3, /device:TPU:1, one launch (start us, length us, event | category | flops | bytes accessed | tf_op | source)
XLA Modules:
  0.0 67.6 jit_solution(6375060321920845371)
XLA Ops:
  0.6 60.2 %shard_map.135 = (bf16[2048,2048]{1,0:T(8,128)(2,1)S(1)}, bf16[2048,2048]{1,0:T(8,128)(2,1)S(1)}, f32[2,64,2048]{2,1,0:T(8,128)S(1)}, f32[2,1,4096]{2,1,0:T(1,128)S(1)}) custom-call(f32[64,2048]{1,0:T(8,128)} %wg.1, f32[64,2048]{1,0:T(8,128)} %mg.1, f32[64,2048]{1,0:T(8,128)} %sg.1, f32[64,2048]{1,0:T(8,128)} %wu.1, f32[64,2048]{1,0:T(8,128)} %mu.1, ...), custom_call_target="tpu_custom_call" | custom-call | tf_op jit(solution)/shard_map/pallas_call | solution.py:329
  60.8 6.8 %shard_map.136 = (bf16[2048,2048]{1,0:T(8,128)(2,1)}, bf16[2048,2048]{1,0:T(8,128)(2,1)}, f32[1,2048]{1,0:T(1,128)}, f32[1,2048]{1,0:T(1,128)}, bf16[2048]{0:T(1...) custom-call(bf16[2048,2048]{1,0:T(8,128)(2,1)S(1)} %get-tuple-element.18.big_g, ...), custom_call_target="tpu_custom_call" | custom-call | tf_op jit(solution)/shard_map/pallas_call | solution.py:364

commit v4 on v3

--- a/solution.py
+++ b/solution.py
@@ -52,6 +52,10 @@
     return 0 if step == 1 else CUTS - 1
 
 
+def rest(array, step, part):
+    return (part + part // 2, part // 2) if step == 1 else (0, part // 2)
+
+
 def starts():
     for turn in (0, 1):
         for position in range(CUTS):
@@ -70,7 +74,8 @@
 
     def send(chunk, axis, step, turn, now):
         array, first, second, cut = chunk
-        done = max(free.get((axis, step), 0.0), now) + span
+        own_rest = turn == 0 and first == 0
+        done = max(free.get((axis, step), 0.0), now) + (span / 2 if own_rest else span)
         free[axis, step] = done
         heapq.heappush(queue, (done + delay, (array, *moved(first, second, turn, step), cut)))
 
@@ -90,7 +95,7 @@
 def kernel(
     wg, mg, sg, wu, mu, su, norm_train, norm_step,
     big_g, big_u, whole, scales,
-    w_in, m_in, s_in, local_max, y_buf, z_buf, ahead, norm_in, norm_row, norm_x, norm_y,
+    loaded, local_max, y_buf, z_buf, ahead, norm_in, norm_row, norm_x, norm_y,
     in_sem, small_send, small_recv, ahead_send, ahead_recv, ring_send, ring_recv, core_sem,
 ):
     rows, columns = wg.shape
@@ -117,41 +122,37 @@
         + x_peers
     )
 
-    inputs = ((wg, mg, sg), (wu, mu, su))
-    loads = [
-        [
-            pltpu.make_async_copy(src, dst.at[a], in_sem.at[3 * a + k])
-            for k, (src, dst) in enumerate(zip(inputs[a], (w_in, m_in, s_in)))
-        ]
-        for a in (0, 1)
-    ]
-    norms = [
-        pltpu.make_async_copy(src, norm_in.at[k], in_sem.at[6 + k])
-        for k, src in enumerate((norm_train, norm_step))
-    ]
-    for copy in loads[0] + loads[1] + norms:
-        copy.start()
+    half = columns // 2
+    for a, refs in enumerate(((wg, mg, sg), (wu, mu, su))):
+        for h in (0, 1):
+            at = pl.ds(h * half, half)
+            for k, src in enumerate(refs):
+                pltpu.make_async_copy(src.at[:, at], loaded.at[k, a, :, at], in_sem.at[2 * a + h]).start()
+    for k, src in enumerate((norm_train, norm_step)):
+        pltpu.make_async_copy(src, norm_in.at[k], in_sem.at[4]).start()
 
     barrier = pltpu.get_barrier_semaphore()
     for peer in peers:
         pl.semaphore_signal(barrier, inc=1, device_id=peer, device_id_type=MESH)
 
+    def await_bytes(ref, sem):
+        pltpu.make_async_copy(ref, ref, sem).wait()
+
     for a in (0, 1):
-        for copy in loads[a]:
-            copy.wait()
-
-        @pl.loop(0, columns // LANES)
-        def _(j):
-            at = pl.ds(pl.multiple_of(j * LANES, LANES), LANES)
-            weight = w_in[a, :, at]
-            new = weight - learn_rate * (
-                m_in[a, :, at] / (jnp.sqrt(s_in[a, :, at]) + tiny_value) + decay_rate * weight
-            )
-            whole[a, :, at] = new
-            local_max[a, :, at] = jnp.max(jnp.abs(new), axis=0, keepdims=True)
-
-    for copy in norms:
-        copy.wait()
+        for h in (0, 1):
+            await_bytes(loaded.at[:, a, :, pl.ds(h * half, half)], in_sem.at[2 * a + h])
+
+            @pl.loop(0, half // LANES)
+            def _(j):
+                at = pl.ds(pl.multiple_of(h * half + j * LANES, LANES), LANES)
+                weight, moment, square = (loaded[k, a, :, at] for k in range(3))
+                new = weight - learn_rate * (
+                    moment / (jnp.sqrt(square) + tiny_value) + decay_rate * weight
+                )
+                whole[a, :, at] = new
+                local_max[a, :, at] = jnp.max(jnp.abs(new), axis=0, keepdims=True)
+
+    await_bytes(norm_in, in_sem.at[4])
     gain = norm_in[0] + norm_in[1]
     for k in range(8):
         norm_row[:, 16 * k : 16 * (k + 1)] = gain
@@ -174,29 +175,26 @@
     def small(stage, src, dst, peer):
         send(src, dst, small_send.at[stage], small_recv.at[stage], peer)
 
-    def await_bytes(ref, sem):
-        pltpu.make_async_copy(ref, ref, sem).wait()
-
     for k, flip in steps:
         a = 1 - core if flip else core
         small(0, local_max.at[a], y_buf.at[2 * ((SIDE - k) % SIDE) + flip - 1], (device(dy=k, flip=flip), x))
 
-    def send_ahead(array, step, half):
-        cut, slot = early(array, step), 2 * array + (step == -1)
-        size = part // 2
-        send(
-            whole.at[array, pl.ds(cut * part + half * size, size)],
-            ahead.at[slot, pl.ds(half * size, size)],
-            ahead_send,
-            ahead_recv.at[slot],
-            near(array, step),
-        )
-
-    for step in (1, -1):
-        send_ahead(1, step, 0)
-    for half in (0, 1):
+    def send_ahead(array, low, high, late):
         for step in (1, -1):
-            send_ahead(0, step, half)
+            side = int(step == -1)
+            where = pl.ds(low if step == 1 else rows - high, high - low)
+            send(
+                whole.at[array, where],
+                ahead.at[side, array, where],
+                ahead_send,
+                ahead_recv.at[2 * side + late],
+                near(array, step),
+            )
+
+    send_ahead(1, 0, part // 2, 0)
+    send_ahead(1, part // 2, 3 * part // 4, 0)
+    send_ahead(0, 0, part, 0)
+    send_ahead(0, part, 3 * part // 2, 1)
     for k, peer in enumerate(x_peers):
         small(2, norm_x.at[3], norm_x.at[k], peer)
     await_bytes(y_buf, small_recv.at[0])
@@ -209,75 +207,121 @@
     z_buf[here, :, columns:] = norm_x[0] + norm_x[1] + norm_x[2] + norm_x[3]
     for k, flip in steps:
         small(1, z_buf.at[here], z_buf.at[here], (device(dz=k, flip=flip), x))
-    for step in (1, -1):
-        send_ahead(1, step, 1)
+    send_ahead(1, 3 * part // 4, part, 0)
+    send_ahead(1, part, 3 * part // 2, 1)
     await_bytes(z_buf.at[pl.ds(0, 7)], small_recv.at[1])
 
     big = (big_g, big_u)
     own = pl.multiple_of(me * rows, rows)
-    for a in (0, 1):
-        first = SIDE * a
-
+
+    def scaled(array, src, start, base, size, at):
+        factor = 1.0 / scales[array, :, at]
+        there = pl.ds(pl.multiple_of(base + start, size), size)
+        big[array][there, at] = (src[pl.ds(start, size), at] * factor).astype(jnp.bfloat16)
+
+    def blocks(work):
         @pl.loop(0, columns // LANES)
         def _(j):
-            at = pl.ds(pl.multiple_of(j * LANES, LANES), LANES)
-            best = jnp.maximum(
+            work(pl.ds(pl.multiple_of(j * LANES, LANES), LANES))
+
+    def open_piece(at):
+        for a in (0, 1):
+            first = SIDE * a
+            scales[a, :, at] = jnp.maximum(
                 jnp.maximum(z_buf[first, :, at], z_buf[first + 1, :, at]),
                 jnp.maximum(z_buf[first + 2, :, at], z_buf[first + 3, :, at]),
             )
-            scales[a, :, at] = best
-            factor = 1.0 / best
-            big[a][pl.ds(own, rows), at] = (whole[a, :, at] * factor).astype(jnp.bfloat16)
-
+            for step in (1, -1):
+                start, size = rest(a, step, part)
+                scaled(a, whole.at[a], start, own, size, at)
+
+    def close_piece(at):
+        for a in (0, 1):
+            for start in (part // 2, part):
+                scaled(a, whole.at[a], start, own, part // 2, at)
+
+    blocks(open_piece)
+
+    names = {}
+
+    def arrival(first, second, cut, piece=0):
+        return ring_recv.at[names.setdefault((first, second, cut, piece), len(names))]
+
+    def start_of(array, first, second):
+        dy, dz = (first, second) if array == 0 else (second, first)
+        return device(dz=dz, dy=dy) * rows
+
+    def span(array, first, second, start, size):
+        at = start_of(array, first, second) + start
+        return big[array].at[pl.ds(pl.multiple_of(at, size), size)]
+
+    def parts_of(first, second, cut):
+        pieces = 2 if first == 2 and second == 2 else 1
+        size = part // pieces
+        return [(cut * part + k * size, size) for k in range(pieces)]
+
+    def pass_on(chunk, axis, step, turn):
+        array, first, second, cut = chunk
+        there = (*moved(first, second, turn, step), cut)
+        copies = [rest(array, step, part)] if turn == 0 and first == 0 else parts_of(*there)
+        for k, (start, size) in enumerate(copies):
+            piece = span(array, first, second, start, size)
+            send(piece, piece, ring_send, arrival(*there, k), near(axis, step))
+
+    def cross(array, first, second, start, size):
+        piece = span(array, first, second, start, size)
+        send(piece, piece, core_sem.at[0], core_sem.at[1], partner)
+
+    openings = list(starts())
+    for chunk, axis, step, turn in openings:
+        if turn == 0:
+            pass_on(chunk, axis, step, turn)
+    blocks(close_piece)
+    for chunk, axis, step, turn in openings:
+        if turn == 1:
+            pass_on(chunk, axis, step, turn)
     for k in range(SIDE):
         norm_y[y, :, k * LANES : (k + 1) * LANES] = z_buf[k, :, columns:] + z_buf[SIDE + k, :, columns:]
     for k in (1, 2, 3):
         small(3, norm_y.at[y], norm_y.at[y], (device(dy=k), x))
-
-    names = {}
-
-    def number(chunk):
-        return names.setdefault(chunk, len(names))
-
-    def place(chunk):
-        array, first, second, cut = chunk
-        dy, dz = (first, second) if array == 0 else (second, first)
-        start = device(dz=dz, dy=dy) * rows + cut * part
-        return pl.ds(pl.multiple_of(start, part), part)
-
-    def pass_on(chunk, axis, step, turn):
-        array, first, second, cut = chunk
-        there = (array, *moved(first, second, turn, step), cut)
-        piece = big[array].at[place(chunk)]
-        send(piece, piece, ring_send, ring_recv.at[number(there)], near(axis, step))
-
-    def cross(chunk):
-        piece = big[chunk[0]].at[place(chunk)]
-        send(piece, piece, core_sem.at[0], core_sem.at[1], partner)
-
-    for chunk, axis, step, turn in starts():
-        pass_on(chunk, axis, step, turn)
     for array in (0, 1):
         for cut in range(CUTS):
-            cross((array, 0, 0, cut))
-    for chunk, came_early in arrivals():
-        array, first, second, cut = chunk
+            cross(array, 0, 0, cut * part, part)
+
+    def from_ahead(side, first, start, size):
+        def work(at):
+            for array in (0, 1):
+                scaled(array, ahead.at[side, array], start, start_of(array, first, 0), size, at)
+
+        blocks(work)
+
+    last = []
+    for (array, first, second, cut), came_early in arrivals():
+        if array == 1:
+            continue
+        if (first, second) == (2, 2):
+            last.append(cut)
+            continue
+        side, size = int(first == 1), part // 2
         if came_early:
-            slot = 2 * array + (first == 1)
-            await_bytes(ahead.at[slot], ahead_recv.at[slot])
-            where = place(chunk)
-
-            @pl.loop(0, columns // LANES)
-            def _(j):
-                at = pl.ds(pl.multiple_of(j * LANES, LANES), LANES)
-                factor = 1.0 / scales[array, :, at]
-                big[array][where, at] = (ahead[slot, :, at] * factor).astype(jnp.bfloat16)
-
+            await_bytes(ahead.at[side, :, pl.ds(0, part)], ahead_recv.at[2 * side])
+            from_ahead(side, first, cut * part, part)
+        elif second == 0 and first in (1, -1):
+            await_bytes(ahead.at[side, :, pl.ds(0, size)], ahead_recv.at[2 * side + 1])
+            from_ahead(side, first, size if first == 1 else part, size)
+            await_bytes(big_g.at[pl.ds(0, 2 * size)], arrival(first, second, cut))
         else:
-            await_bytes(big[array].at[place(chunk)], ring_recv.at[number(chunk)])
-        for axis, step, turn in onward(*chunk):
-            pass_on(chunk, axis, step, turn)
-        cross(chunk)
+            await_bytes(big_g.at[pl.ds(0, 2 * part)], arrival(first, second, cut))
+        for a in (0, 1):
+            for axis, step, turn in onward(a, first, second, cut):
+                pass_on((a, first, second, cut), axis, step, turn)
+            cross(a, first, second, cut * part, part)
+    for k in (0, 1):
+        for cut in last:
+            start, size = parts_of(2, 2, cut)[k]
+            await_bytes(big_g.at[pl.ds(0, 2 * size)], arrival(2, 2, cut, k))
+            for a in (0, 1):
+                cross(a, 2, 2, start, size)
 
     await_bytes(norm_y.at[pl.ds(0, 3)], small_recv.at[3])
     for k in range(SIDE):
@@ -288,8 +332,8 @@
     await_bytes(z_buf.at[pl.ds(0, 7)], small_send.at[1])
     await_bytes(norm_x.at[pl.ds(0, 3)], small_send.at[2])
     await_bytes(norm_y.at[pl.ds(0, 3)], small_send.at[3])
-    await_bytes(whole, ahead_send)
-    passed = 2 * CUTS * (SIDE * SIDE - 1) - 4
+    await_bytes(ahead.at[:, :, pl.ds(0, 3 * part // 2)], ahead_send)
+    passed = 2 * CUTS * (SIDE * SIDE - 1) - 6
     await_bytes(big_g.at[pl.ds(0, passed * part)], ring_send)
     await_bytes(big_g, core_sem.at[0])
     await_bytes(big_u, core_sem.at[1])
@@ -297,7 +341,7 @@
 
 def deliver(
     big_g, big_u, whole, scales,
-    serving_g, serving_u, scale_g, scale_u, serve_norm, whole_g, whole_u, sem,
+    serving_g, serving_u, scale_g, scale_u, serve_norm, whole_g, whole_u, norm, sem,
 ):
     columns = big_g.shape[1]
     copies = []
@@ -306,15 +350,16 @@
         copies.append(pltpu.make_async_copy(src, dst, sem.at[len(copies)]))
         copies[-1].start()
 
+    norm[...] = scales[0, :, columns:].astype(jnp.bfloat16).reshape(-1)
+    put(scales.at[0, :, pl.ds(0, columns)], scale_g)
+    put(scales.at[1, :, pl.ds(0, columns)], scale_u)
+    put(whole.at[0], whole_g)
+    put(whole.at[1], whole_u)
     step = big_g.shape[0] // PARTS
     for src, dst in ((big_g, serving_g), (big_u, serving_u)):
         for k in range(PARTS):
             put(src.at[pl.ds(k * step, step)], dst.at[pl.ds(k * step, step)])
-    put(whole.at[0], whole_g)
-    put(whole.at[1], whole_u)
-    scale_g[...] = scales[0, :, 0:columns]
-    scale_u[...] = scales[1, :, 0:columns]
-    serve_norm[...] = scales[0, :, columns:].astype(jnp.bfloat16).reshape(-1)
+    put(norm, serve_norm)
     for copy in copies:
         copy.wait()
 
@@ -322,7 +367,7 @@
 def body(wg, mg, sg, wu, mu, su, norm_train, norm_step):
     rows, columns = wg.shape
     total = rows * lax.axis_size("shard")
-    chunks = 2 * CUTS * (SIDE * SIDE - 1) - 4
+    chunks = CUTS * (SIDE * SIDE - 1)
     f32, bf16 = jnp.float32, jnp.bfloat16
     hbm, vmem = pl.BlockSpec(memory_space=pltpu.HBM), pl.BlockSpec(memory_space=pltpu.VMEM)
     dma = pltpu.SemaphoreType.DMA
@@ -337,18 +382,16 @@
         in_specs=[hbm] * 8,
         out_specs=(vmem,) * 4,
         scratch_shapes=[
-            pltpu.VMEM((2, rows, columns), f32),
-            pltpu.VMEM((2, rows, columns), f32),
-            pltpu.VMEM((2, rows, columns), f32),
+            pltpu.VMEM((3, 2, rows, columns), f32),
             pltpu.VMEM((2, 1, columns), f32),
             pltpu.VMEM((7, 1, columns), f32),
             pltpu.VMEM((2 * SIDE, 1, columns + LANES), f32),
-            pltpu.VMEM((4, rows // CUTS, columns), f32),
+            pltpu.VMEM((2, 2, rows, columns), f32),
             pltpu.VMEM((2, 1, 16), f32),
             pltpu.VMEM((1, LANES), f32),
             pltpu.VMEM((SIDE, 1, LANES), f32),
             pltpu.VMEM((SIDE, 1, SIDE * LANES), f32),
-            dma((8,)),
+            dma((5,)),
             dma((4,)),
             dma((4,)),
             dma,
@@ -373,8 +416,8 @@
             jax.ShapeDtypeStruct((rows, columns), f32),
         ),
         in_specs=[vmem] * 4,
-        out_specs=(hbm, hbm, vmem, vmem, vmem, hbm, hbm),
-        scratch_shapes=[dma((2 * PARTS + 2,))],
+        out_specs=(hbm,) * 7,
+        scratch_shapes=[pltpu.VMEM((total,), bf16), dma((2 * PARTS + 5,))],
         compiler_params=pltpu.CompilerParams(vmem_limit_bytes=24 * 1024 * 1024),
     )(*gathered)
     return (

time: 67.7 us -> 66.2 us (0.978)
  Pallas kernels: 67 us -> 65.4 us
    pallas_call x1, Pallas kernels: 60.2 us -> 59.1 us  [body(): pl.pallas_call(kernel, out_shape=(pltpu.VMEM((total, columns), bf16), plt...]
where the time goes in v4:
time: 66.2 us; the launch traced here: 66.1 us
  Pallas kernels  65.4 us (99%)
    pallas_call x1, Pallas kernels, body(): pl.pallas_call(kernel, out_shape=(pltpu.VMEM((total, columns), bf16), plt...  59.1 us
    pallas_call x1, Pallas kernels, body(): pl.pallas_call(deliver, out_shape=(jax.ShapeDtypeStruct((total, columns),...  6.35 us

profile of v4, /device:TPU:1, one launch (start us, length us, event | category | flops | bytes accessed | tf_op | source)
XLA Modules:
  0.0 66.1 jit_solution(10878615342420373729)
XLA Ops:
  0.6 59.1 %shard_map.135 = (bf16[2048,2048]{1,0:T(8,128)(2,1)S(1)}, bf16[2048,2048]{1,0:T(8,128)(2,1)S(1)}, f32[2,64,2048]{2,1,0:T(8,128)S(1)}, f32[2,1,4096]{2,1,0:T(1,128)S(1)}) custom-call(f32[64,2048]{1,0:T(8,128)} %wg.1, f32[64,2048]{1,0:T(8,128)} %mg.1, f32[64,2048]{1,0:T(8,128)} %sg.1, f32[64,2048]{1,0:T(8,128)} %wu.1, f32[64,2048]{1,0:T(8,128)} %mu.1, ...), custom_call_target="tpu_custom_call" | custom-call | tf_op jit(solution)/shard_map/pallas_call | solution.py:374
  59.7 6.4 %shard_map.136 = (bf16[2048,2048]{1,0:T(8,128)(2,1)}, bf16[2048,2048]{1,0:T(8,128)(2,1)}, f32[1,2048]{1,0:T(1,128)}, f32[1,2048]{1,0:T(1,128)}, bf16[2048]{0:T(1...) custom-call(bf16[2048,2048]{1,0:T(8,128)(2,1)S(1)} %get-tuple-element.18.big_g, ...), custom_call_target="tpu_custom_call" | custom-call | tf_op jit(solution)/shard_map/pallas_call | solution.py:407

commit v5 on v4

--- a/solution.py
+++ b/solution.py
@@ -16,7 +16,11 @@
 SIDE = 4
 CUTS = 2
 LANES = 128
+UNROLL = 4
 PARTS = 2
+AHEAD = 48
+FIRST = 24
+REST = 0.5
 
 
 def axis_of(array, turn):
@@ -53,7 +57,7 @@
 
 
 def rest(array, step, part):
-    return (part + part // 2, part // 2) if step == 1 else (0, part // 2)
+    return (AHEAD, 2 * part - AHEAD) if step == 1 else (0, 2 * part - AHEAD)
 
 
 def starts():
@@ -75,7 +79,7 @@
     def send(chunk, axis, step, turn, now):
         array, first, second, cut = chunk
         own_rest = turn == 0 and first == 0
-        done = max(free.get((axis, step), 0.0), now) + (span / 2 if own_rest else span)
+        done = max(free.get((axis, step), 0.0), now) + (REST if own_rest else span)
         free[axis, step] = done
         heapq.heappush(queue, (done + delay, (array, *moved(first, second, turn, step), cut)))
 
@@ -95,8 +99,8 @@
 def kernel(
     wg, mg, sg, wu, mu, su, norm_train, norm_step,
     big_g, big_u, whole, scales,
-    loaded, local_max, y_buf, z_buf, ahead, norm_in, norm_row, norm_x, norm_y,
-    in_sem, small_send, small_recv, ahead_send, ahead_recv, ring_send, ring_recv, core_sem,
+    loaded, local_max, y_buf, z_buf, ahead, norm_in, norm_row, norm_z, norm_x, norm_y,
+    in_sem, small_send, small_recv, norm_send, norm_recv, ahead_send, ahead_recv, ring_send, ring_recv, core_sem,
 ):
     rows, columns = wg.shape
     part = rows // CUTS
@@ -116,11 +120,9 @@
     partner = (device(flip=1), x)
     steps = [(k, flip) for k in (2, 1, 3) for flip in (0, 1)] + [(0, 1)]
     x_peers = [(me, lax.rem(x + k, SIDE)) for k in (1, 2, 3)]
-    peers = (
-        [(device(dy=k, flip=f), x) for k, f in steps]
-        + [(device(dz=k, flip=f), x) for k, f in steps if k]
-        + x_peers
-    )
+    y_peers = [(device(dy=k, flip=f), x) for k, f in steps]
+    z_peers = [(device(dz=k, flip=f), x) for k, f in steps]
+    peers = y_peers + z_peers[:-1]
 
     half = columns // 2
     for a, refs in enumerate(((wg, mg, sg), (wu, mu, su))):
@@ -135,6 +137,11 @@
     for peer in peers:
         pl.semaphore_signal(barrier, inc=1, device_id=peer, device_id_type=MESH)
 
+    @pl.when(z == 0)
+    def _():
+        for peer in x_peers:
+            pl.semaphore_signal(barrier, inc=1, device_id=peer, device_id_type=MESH)
+
     def await_bytes(ref, sem):
         pltpu.make_async_copy(ref, ref, sem).wait()
 
@@ -142,13 +149,12 @@
         for h in (0, 1):
             await_bytes(loaded.at[:, a, :, pl.ds(h * half, half)], in_sem.at[2 * a + h])
 
-            @pl.loop(0, half // LANES)
+            @pl.loop(0, half // LANES, unroll=UNROLL)
             def _(j):
                 at = pl.ds(pl.multiple_of(h * half + j * LANES, LANES), LANES)
                 weight, moment, square = (loaded[k, a, :, at] for k in range(3))
-                new = weight - learn_rate * (
-                    moment / (jnp.sqrt(square) + tiny_value) + decay_rate * weight
-                )
+                root = square * lax.rsqrt(square) + tiny_value
+                new = weight * (1.0 - learn_rate * decay_rate) - (learn_rate * moment) / root
                 whole[a, :, at] = new
                 local_max[a, :, at] = jnp.max(jnp.abs(new), axis=0, keepdims=True)
 
@@ -158,9 +164,9 @@
         norm_row[:, 16 * k : 16 * (k + 1)] = gain
     lane = lax.broadcasted_iota(jnp.int32, (1, LANES), 1)
     mine = lax.div(lane, 16) == core * SIDE + x
-    norm_x[3] = jnp.where(mine, norm_row[...], 0.0)
-
-    pl.semaphore_wait(barrier, len(peers))
+    norm_z[z] = jnp.where(mine, norm_row[...], 0.0)
+
+    pl.semaphore_wait(barrier, len(peers) + len(x_peers) * lax.div(SIDE - z, SIDE))
 
     def send(src, dst, send_sem, recv_sem, peer):
         pltpu.make_async_remote_copy(
@@ -178,6 +184,42 @@
     for k, flip in steps:
         a = 1 - core if flip else core
         small(0, local_max.at[a], y_buf.at[2 * ((SIDE - k) % SIDE) + flip - 1], (device(dy=k, flip=flip), x))
+
+    def gain(stage, src, dst, peer):
+        send(src, dst, norm_send.at[stage], norm_recv.at[stage], peer)
+
+    norm_whole = scales.at[0, :, pl.ds(columns, SIDE * SIDE * LANES)]
+
+    def gain_over_x():
+        @pl.when(z == 0)
+        def _():
+            await_bytes(norm_z.at[pl.ds(0, 3)], norm_recv.at[0])
+            for k, peer in enumerate(x_peers):
+                gain(1, norm_z, norm_x.at[k], peer)
+
+    def gain_over_y():
+        @pl.when(z == 0)
+        def _():
+            await_bytes(norm_x, norm_recv.at[1])
+            slot = SIDE * core + y
+            norm_y[slot] = norm_z[...] + norm_x[0] + norm_x[1] + norm_x[2]
+            for peer in y_peers:
+                gain(2, norm_y.at[slot], norm_y.at[slot], peer)
+
+    def gain_over_z():
+        @pl.when(z == 0)
+        def _():
+            await_bytes(norm_y.at[pl.ds(0, 7)], norm_recv.at[2])
+            for k in range(SIDE):
+                for i in range(SIDE):
+                    at = columns + (k * SIDE + i) * LANES
+                    scales[0, :, at : at + LANES] = norm_y[i, k] + norm_y[SIDE + i, k]
+            for k in (1, 2, 3):
+                gain(3, norm_whole, norm_whole, (device(dz=k), x))
+
+    @pl.when(z > 0)
+    def _():
+        gain(0, norm_z.at[z], norm_z.at[z], (device(dz=-z), x))
 
     def send_ahead(array, low, high, late):
         for step in (1, -1):
@@ -191,24 +233,19 @@
                 near(array, step),
             )
 
-    send_ahead(1, 0, part // 2, 0)
-    send_ahead(1, part // 2, 3 * part // 4, 0)
+    send_ahead(1, 0, FIRST, 0)
     send_ahead(0, 0, part, 0)
-    send_ahead(0, part, 3 * part // 2, 1)
-    for k, peer in enumerate(x_peers):
-        small(2, norm_x.at[3], norm_x.at[k], peer)
+    send_ahead(0, part, AHEAD, 1)
     await_bytes(y_buf, small_recv.at[0])
     best = local_max[core]
     for k in range(7):
         best = jnp.maximum(best, y_buf[k])
-    await_bytes(norm_x.at[pl.ds(0, 3)], small_recv.at[2])
     here = SIDE * core + z
-    z_buf[here, :, 0:columns] = best
-    z_buf[here, :, columns:] = norm_x[0] + norm_x[1] + norm_x[2] + norm_x[3]
+    z_buf[here] = best
     for k, flip in steps:
         small(1, z_buf.at[here], z_buf.at[here], (device(dz=k, flip=flip), x))
-    send_ahead(1, 3 * part // 4, part, 0)
-    send_ahead(1, part, 3 * part // 2, 1)
+    send_ahead(1, FIRST, part, 0)
+    send_ahead(1, part, AHEAD, 1)
     await_bytes(z_buf.at[pl.ds(0, 7)], small_recv.at[1])
 
     big = (big_g, big_u)
@@ -216,11 +253,11 @@
 
     def scaled(array, src, start, base, size, at):
         factor = 1.0 / scales[array, :, at]
-        there = pl.ds(pl.multiple_of(base + start, size), size)
+        there = pl.ds(pl.multiple_of(base + start, 8), size)
         big[array][there, at] = (src[pl.ds(start, size), at] * factor).astype(jnp.bfloat16)
 
     def blocks(work):
-        @pl.loop(0, columns // LANES)
+        @pl.loop(0, columns // LANES, unroll=UNROLL)
         def _(j):
             work(pl.ds(pl.multiple_of(j * LANES, LANES), LANES))
 
@@ -237,8 +274,7 @@
 
     def close_piece(at):
         for a in (0, 1):
-            for start in (part // 2, part):
-                scaled(a, whole.at[a], start, own, part // 2, at)
+            scaled(a, whole.at[a], 2 * part - AHEAD, own, 2 * AHEAD - 2 * part, at)
 
     blocks(open_piece)
 
@@ -253,7 +289,7 @@
 
     def span(array, first, second, start, size):
         at = start_of(array, first, second) + start
-        return big[array].at[pl.ds(pl.multiple_of(at, size), size)]
+        return big[array].at[pl.ds(pl.multiple_of(at, 8), size)]
 
     def parts_of(first, second, cut):
         pieces = 2 if first == 2 and second == 2 else 1
@@ -280,10 +316,7 @@
     for chunk, axis, step, turn in openings:
         if turn == 1:
             pass_on(chunk, axis, step, turn)
-    for k in range(SIDE):
-        norm_y[y, :, k * LANES : (k + 1) * LANES] = z_buf[k, :, columns:] + z_buf[SIDE + k, :, columns:]
-    for k in (1, 2, 3):
-        small(3, norm_y.at[y], norm_y.at[y], (device(dy=k), x))
+    gain_over_x()
     for array in (0, 1):
         for cut in range(CUTS):
             cross(array, 0, 0, cut * part, part)
@@ -302,20 +335,24 @@
         if (first, second) == (2, 2):
             last.append(cut)
             continue
-        side, size = int(first == 1), part // 2
+        side, size, left = int(first == 1), AHEAD - part, 2 * part - AHEAD
         if came_early:
             await_bytes(ahead.at[side, :, pl.ds(0, part)], ahead_recv.at[2 * side])
             from_ahead(side, first, cut * part, part)
         elif second == 0 and first in (1, -1):
             await_bytes(ahead.at[side, :, pl.ds(0, size)], ahead_recv.at[2 * side + 1])
-            from_ahead(side, first, size if first == 1 else part, size)
-            await_bytes(big_g.at[pl.ds(0, 2 * size)], arrival(first, second, cut))
+            from_ahead(side, first, left if first == 1 else part, size)
+            await_bytes(big_g.at[pl.ds(0, 2 * left)], arrival(first, second, cut))
+            if first == 1:
+                gain_over_y()
         else:
             await_bytes(big_g.at[pl.ds(0, 2 * part)], arrival(first, second, cut))
         for a in (0, 1):
             for axis, step, turn in onward(a, first, second, cut):
                 pass_on((a, first, second, cut), axis, step, turn)
             cross(a, first, second, cut * part, part)
+        if (first, second, cut) == (-1, 1, 1):
+            gain_over_z()
     for k in (0, 1):
         for cut in last:
             start, size = parts_of(2, 2, cut)[k]
@@ -323,18 +360,22 @@
             for a in (0, 1):
                 cross(a, 2, 2, start, size)
 
-    await_bytes(norm_y.at[pl.ds(0, 3)], small_recv.at[3])
-    for k in range(SIDE):
-        for i in range(SIDE):
-            at = columns + (k * SIDE + i) * LANES
-            scales[0, :, at : at + LANES] = norm_y[i, :, k * LANES : (k + 1) * LANES]
+    @pl.when(z > 0)
+    def _():
+        await_bytes(norm_whole, norm_recv.at[3])
+        await_bytes(norm_z.at[0], norm_send.at[0])
+
+    @pl.when(z == 0)
+    def _():
+        await_bytes(norm_x, norm_send.at[1])
+        await_bytes(norm_y.at[pl.ds(0, 7)], norm_send.at[2])
+        await_bytes(y_buf.at[pl.ds(0, 3)], norm_send.at[3])
+
     await_bytes(y_buf, small_send.at[0])
     await_bytes(z_buf.at[pl.ds(0, 7)], small_send.at[1])
-    await_bytes(norm_x.at[pl.ds(0, 3)], small_send.at[2])
-    await_bytes(norm_y.at[pl.ds(0, 3)], small_send.at[3])
-    await_bytes(ahead.at[:, :, pl.ds(0, 3 * part // 2)], ahead_send)
-    passed = 2 * CUTS * (SIDE * SIDE - 1) - 6
-    await_bytes(big_g.at[pl.ds(0, passed * part)], ring_send)
+    await_bytes(ahead.at[:, :, pl.ds(0, AHEAD)], ahead_send)
+    passed = 2 * (SIDE * SIDE - 1) * rows - 4 * AHEAD
+    await_bytes(big_g.at[pl.ds(0, passed)], ring_send)
     await_bytes(big_g, core_sem.at[0])
     await_bytes(big_u, core_sem.at[1])
 
@@ -350,15 +391,15 @@
         copies.append(pltpu.make_async_copy(src, dst, sem.at[len(copies)]))
         copies[-1].start()
 
-    norm[...] = scales[0, :, columns:].astype(jnp.bfloat16).reshape(-1)
-    put(scales.at[0, :, pl.ds(0, columns)], scale_g)
-    put(scales.at[1, :, pl.ds(0, columns)], scale_u)
-    put(whole.at[0], whole_g)
-    put(whole.at[1], whole_u)
     step = big_g.shape[0] // PARTS
     for src, dst in ((big_g, serving_g), (big_u, serving_u)):
         for k in range(PARTS):
             put(src.at[pl.ds(k * step, step)], dst.at[pl.ds(k * step, step)])
+    put(whole.at[0], whole_g)
+    put(whole.at[1], whole_u)
+    put(scales.at[0, :, pl.ds(0, columns)], scale_g)
+    put(scales.at[1, :, pl.ds(0, columns)], scale_u)
+    norm[...] = scales[0, :, columns:].astype(jnp.bfloat16).reshape(-1)
     put(norm, serve_norm)
     for copy in copies:
         copy.wait()
@@ -385,13 +426,16 @@
             pltpu.VMEM((3, 2, rows, columns), f32),
             pltpu.VMEM((2, 1, columns), f32),
             pltpu.VMEM((7, 1, columns), f32),
-            pltpu.VMEM((2 * SIDE, 1, columns + LANES), f32),
+            pltpu.VMEM((2 * SIDE, 1, columns), f32),
             pltpu.VMEM((2, 2, rows, columns), f32),
             pltpu.VMEM((2, 1, 16), f32),
             pltpu.VMEM((1, LANES), f32),
             pltpu.VMEM((SIDE, 1, LANES), f32),
-            pltpu.VMEM((SIDE, 1, SIDE * LANES), f32),
+            pltpu.VMEM((3, SIDE, 1, LANES), f32),
+            pltpu.VMEM((2 * SIDE, SIDE, 1, LANES), f32),
             dma((5,)),
+            dma((2,)),
+            dma((2,)),
             dma((4,)),
             dma((4,)),
             dma,

time: 66.2 us -> 65.5 us (0.989)
  Pallas kernels: 65.4 us -> 64.7 us
where the time goes in v5:
time: 65.5 us; the launch traced here: 65.3 us
  Pallas kernels  64.7 us (99%)
    pallas_call x1, Pallas kernels, body(): pl.pallas_call(kernel, out_shape=(pltpu.VMEM((total, columns), bf16), plt...  58.5 us
    pallas_call x1, Pallas kernels, body(): pl.pallas_call(deliver, out_shape=(jax.ShapeDtypeStruct((total, columns),...  6.2 us

profile of v5, /device:TPU:1, one launch (start us, length us, event | category | flops | bytes accessed | tf_op | source)
XLA Modules:
  0.0 65.3 jit_solution(9021816917051240817)
XLA Ops:
  0.6 58.5 %shard_map.135 = (bf16[2048,2048]{1,0:T(8,128)(2,1)S(1)}, bf16[2048,2048]{1,0:T(8,128)(2,1)S(1)}, f32[2,64,2048]{2,1,0:T(8,128)S(1)}, f32[2,1,4096]{2,1,0:T(1,128)S(1)}) custom-call(f32[64,2048]{1,0:T(8,128)} %wg.1, f32[64,2048]{1,0:T(8,128)} %mg.1, f32[64,2048]{1,0:T(8,128)} %sg.1, f32[64,2048]{1,0:T(8,128)} %wu.1, f32[64,2048]{1,0:T(8,128)} %mu.1, ...), custom_call_target="tpu_custom_call" | custom-call | tf_op jit(solution)/shard_map/pallas_call | solution.py:415
  59.1 6.2 %shard_map.136 = (bf16[2048,2048]{1,0:T(8,128)(2,1)}, bf16[2048,2048]{1,0:T(8,128)(2,1)}, f32[1,2048]{1,0:T(1,128)}, f32[1,2048]{1,0:T(1,128)}, bf16[2048]{0:T(1...) custom-call(bf16[2048,2048]{1,0:T(8,128)(2,1)S(1)} %get-tuple-element.18.big_g, ...), custom_call_target="tpu_custom_call" | custom-call | tf_op jit(solution)/shard_map/pallas_call | solution.py:451

commit v6 on v5

--- a/solution.py
+++ b/solution.py
@@ -309,24 +309,51 @@
         send(piece, piece, core_sem.at[0], core_sem.at[1], partner)
 
     openings = list(starts())
-    for chunk, axis, step, turn in openings:
-        if turn == 0:
-            pass_on(chunk, axis, step, turn)
-    blocks(close_piece)
-    for chunk, axis, step, turn in openings:
-        if turn == 1:
-            pass_on(chunk, axis, step, turn)
+
+    def first_sends():
+        for chunk, axis, step, turn in openings:
+            if turn == 0:
+                pass_on(chunk, axis, step, turn)
+        blocks(close_piece)
+        for chunk, axis, step, turn in openings:
+            if turn == 1:
+                pass_on(chunk, axis, step, turn)
+
+    def from_ahead(side, first, start, size):
+        def work(at):
+            for array in (0, 1):
+                scaled(array, ahead.at[side, array], start, start_of(array, first, 0), size, at)
+
+        blocks(work)
+
+    sides = ((0, -1), (1, 1))
+    more, left = AHEAD - part, 2 * part - AHEAD
+
+    def take_early():
+        for side, first in sides:
+            await_bytes(ahead.at[side, :, pl.ds(0, part)], ahead_recv.at[2 * side])
+            from_ahead(side, first, side * part, part)
+
+    def take_late():
+        for side, first in sides:
+            await_bytes(ahead.at[side, :, pl.ds(0, more)], ahead_recv.at[2 * side + 1])
+            from_ahead(side, first, left if side else part, more)
+
+    @pl.when(core == 0)
+    def _():
+        first_sends()
+        take_early()
+
+    @pl.when(core == 1)
+    def _():
+        take_early()
+        take_late()
+        first_sends()
+
     gain_over_x()
     for array in (0, 1):
         for cut in range(CUTS):
             cross(array, 0, 0, cut * part, part)
-
-    def from_ahead(side, first, start, size):
-        def work(at):
-            for array in (0, 1):
-                scaled(array, ahead.at[side, array], start, start_of(array, first, 0), size, at)
-
-        blocks(work)
 
     last = []
     for (array, first, second, cut), came_early in arrivals():
@@ -335,17 +362,13 @@
         if (first, second) == (2, 2):
             last.append(cut)
             continue
-        side, size, left = int(first == 1), AHEAD - part, 2 * part - AHEAD
-        if came_early:
-            await_bytes(ahead.at[side, :, pl.ds(0, part)], ahead_recv.at[2 * side])
-            from_ahead(side, first, cut * part, part)
-        elif second == 0 and first in (1, -1):
-            await_bytes(ahead.at[side, :, pl.ds(0, size)], ahead_recv.at[2 * side + 1])
-            from_ahead(side, first, left if first == 1 else part, size)
+        if second == 0 and first in (1, -1) and not came_early:
+            if first == -1:
+                pl.when(core == 0)(take_late)
             await_bytes(big_g.at[pl.ds(0, 2 * left)], arrival(first, second, cut))
             if first == 1:
                 gain_over_y()
-        else:
+        elif not came_early:
             await_bytes(big_g.at[pl.ds(0, 2 * part)], arrival(first, second, cut))
         for a in (0, 1):
             for axis, step, turn in onward(a, first, second, cut):

time: 65.5 us -> 64.9 us (level)
  no operation moved by 1% of the time
where the time goes in v6:
time: 64.9 us; the launch traced here: 64.8 us
  Pallas kernels  64.2 us (99%)
    pallas_call x1, Pallas kernels, body(): pl.pallas_call(kernel, out_shape=(pltpu.VMEM((total, columns), bf16), plt...  58 us
    pallas_call x1, Pallas kernels, body(): pl.pallas_call(deliver, out_shape=(jax.ShapeDtypeStruct((total, columns),...  6.2 us

profile of v6, /device:TPU:1, one launch (start us, length us, event | category | flops | bytes accessed | tf_op | source)
XLA Modules:
  0.0 64.8 jit_solution(3817965744500557796)
XLA Ops:
  0.6 58.0 %shard_map.135 = (bf16[2048,2048]{1,0:T(8,128)(2,1)S(1)}, bf16[2048,2048]{1,0:T(8,128)(2,1)S(1)}, f32[2,64,2048]{2,1,0:T(8,128)S(1)}, f32[2,1,4096]{2,1,0:T(1,128)S(1)}) custom-call(f32[64,2048]{1,0:T(8,128)} %wg.1, f32[64,2048]{1,0:T(8,128)} %mg.1, f32[64,2048]{1,0:T(8,128)} %sg.1, f32[64,2048]{1,0:T(8,128)} %wu.1, f32[64,2048]{1,0:T(8,128)} %mu.1, ...), custom_call_target="tpu_custom_call" | custom-call | tf_op jit(solution)/shard_map/pallas_call | solution.py:438
  58.6 6.2 %shard_map.136 = (bf16[2048,2048]{1,0:T(8,128)(2,1)}, bf16[2048,2048]{1,0:T(8,128)(2,1)}, f32[1,2048]{1,0:T(1,128)}, f32[1,2048]{1,0:T(1,128)}, bf16[2048]{0:T(1...) custom-call(bf16[2048,2048]{1,0:T(8,128)(2,1)S(1)} %get-tuple-element.18.big_g, ...), custom_call_target="tpu_custom_call" | custom-call | tf_op jit(solution)/shard_map/pallas_call | solution.py:474

commit v7 on v6

--- a/solution.py
+++ b/solution.py
@@ -90,7 +90,7 @@
             heapq.heappush(queue, (0.0, (array, -step, 0, early(array, step))))
     while queue:
         now, chunk = heapq.heappop(queue)
-        order.append((chunk, now == 0.0))
+        order.append((chunk, now))
         for axis, step, turn in onward(*chunk):
             send(chunk, axis, step, turn, now)
     return order
@@ -278,10 +278,16 @@
 
     blocks(open_piece)
 
+    rounds = {}
+    for (array, *chunk), now in arrivals():
+        if array == 0:
+            rounds.setdefault(round(now, 3), []).append(tuple(chunk))
     names = {}
+    for number, (now, chunks) in enumerate(rounds.items()):
+        names.update({chunk: number for chunk in chunks})
 
     def arrival(first, second, cut, piece=0):
-        return ring_recv.at[names.setdefault((first, second, cut, piece), len(names))]
+        return ring_recv.at[names[first, second, cut] + piece]
 
     def start_of(array, first, second):
         dy, dz = (first, second) if array == 0 else (second, first)
@@ -351,37 +357,36 @@
         first_sends()
 
     gain_over_x()
-    for array in (0, 1):
-        for cut in range(CUTS):
-            cross(array, 0, 0, cut * part, part)
-
-    last = []
-    for (array, first, second, cut), came_early in arrivals():
-        if array == 1:
+
+    for now, chunks in rounds.items():
+        if chunks[0][:2] == (2, 2):
             continue
-        if (first, second) == (2, 2):
-            last.append(cut)
-            continue
-        if second == 0 and first in (1, -1) and not came_early:
-            if first == -1:
+        first, second, cut = chunks[0]
+        if now > 0.0:
+            size = part
+            if second == 0 and first in (1, -1):
                 pl.when(core == 0)(take_late)
-            await_bytes(big_g.at[pl.ds(0, 2 * left)], arrival(first, second, cut))
-            if first == 1:
+                size = left
+            await_bytes(big_g.at[pl.ds(0, 2 * size * len(chunks))], arrival(first, second, cut))
+            if size == left:
                 gain_over_y()
-        elif not came_early:
-            await_bytes(big_g.at[pl.ds(0, 2 * part)], arrival(first, second, cut))
-        for a in (0, 1):
-            for axis, step, turn in onward(a, first, second, cut):
-                pass_on((a, first, second, cut), axis, step, turn)
-            cross(a, first, second, cut * part, part)
-        if (first, second, cut) == (-1, 1, 1):
+        for first, second, cut in chunks:
+            for a in (0, 1):
+                for axis, step, turn in onward(a, first, second, cut):
+                    pass_on((a, first, second, cut), axis, step, turn)
+                cross(a, first, second, cut * part, part)
+        if (0, -1, 0) in chunks:
+            for array in (0, 1):
+                for cut in range(CUTS):
+                    cross(array, 0, 0, cut * part, part)
+        if (-1, 1, 1) in chunks:
             gain_over_z()
     for k in (0, 1):
-        for cut in last:
-            start, size = parts_of(2, 2, cut)[k]
-            await_bytes(big_g.at[pl.ds(0, 2 * size)], arrival(2, 2, cut, k))
+        size = parts_of(2, 2, 0)[k][1]
+        await_bytes(big_g.at[pl.ds(0, 2 * size * CUTS)], arrival(2, 2, 0, k))
+        for cut in range(CUTS):
             for a in (0, 1):
-                cross(a, 2, 2, start, size)
+                cross(a, 2, 2, *parts_of(2, 2, cut)[k])
 
     @pl.when(z > 0)
     def _():
@@ -431,7 +436,7 @@
 def body(wg, mg, sg, wu, mu, su, norm_train, norm_step):
     rows, columns = wg.shape
     total = rows * lax.axis_size("shard")
-    chunks = CUTS * (SIDE * SIDE - 1)
+    rounds = len({round(now, 3) for _, now in arrivals()}) + 1
     f32, bf16 = jnp.float32, jnp.bfloat16
     hbm, vmem = pl.BlockSpec(memory_space=pltpu.HBM), pl.BlockSpec(memory_space=pltpu.VMEM)
     dma = pltpu.SemaphoreType.DMA
@@ -464,7 +469,7 @@
             dma,
             dma((4,)),
             dma,
-            dma((chunks,)),
+            dma((rounds,)),
             dma((2,)),
         ],
         compiler_params=pltpu.CompilerParams(

time: 64.9 us -> 64.8 us (level)
  no operation moved by 1% of the time
where the time goes in v7:
time: 64.8 us; the launch traced here: 64.7 us
  Pallas kernels  64 us (99%)
    pallas_call x1, Pallas kernels, body(): pl.pallas_call(kernel, out_shape=(pltpu.VMEM((total, columns), bf16), plt...  57.8 us
    pallas_call x1, Pallas kernels, body(): pl.pallas_call(deliver, out_shape=(jax.ShapeDtypeStruct((total, columns),...  6.2 us

profile of v7, /device:TPU:1, one launch (start us, length us, event | category | flops | bytes accessed | tf_op | source)
XLA Modules:
  0.0 64.7 jit_solution(15541371151074078399)
XLA Ops:
  0.6 57.8 %shard_map.135 = (bf16[2048,2048]{1,0:T(8,128)(2,1)S(1)}, bf16[2048,2048]{1,0:T(8,128)(2,1)S(1)}, f32[2,64,2048]{2,1,0:T(8,128)S(1)}, f32[2,1,4096]{2,1,0:T(1,128)S(1)}) custom-call(f32[64,2048]{1,0:T(8,128)} %wg.1, f32[64,2048]{1,0:T(8,128)} %mg.1, f32[64,2048]{1,0:T(8,128)} %sg.1, f32[64,2048]{1,0:T(8,128)} %wu.1, f32[64,2048]{1,0:T(8,128)} %mu.1, ...), custom_call_target="tpu_custom_call" | custom-call | tf_op jit(solution)/shard_map/pallas_call | solution.py:443
  58.5 6.2 %shard_map.136 = (bf16[2048,2048]{1,0:T(8,128)(2,1)}, bf16[2048,2048]{1,0:T(8,128)(2,1)}, f32[1,2048]{1,0:T(1,128)}, f32[1,2048]{1,0:T(1,128)}, bf16[2048]{0:T(1...) custom-call(bf16[2048,2048]{1,0:T(8,128)(2,1)S(1)} %get-tuple-element.18.big_g, ...), custom_call_target="tpu_custom_call" | custom-call | tf_op jit(solution)/shard_map/pallas_call | solution.py:479

commit v8 on v7

--- a/solution.py
+++ b/solution.py
@@ -16,7 +16,7 @@
 SIDE = 4
 CUTS = 2
 LANES = 128
-UNROLL = 4
+UNROLL = 8
 PARTS = 2
 AHEAD = 48
 FIRST = 24
@@ -118,7 +118,7 @@
         return (device(dy=step) if axis == 0 else device(dz=step), x)
 
     partner = (device(flip=1), x)
-    steps = [(k, flip) for k in (2, 1, 3) for flip in (0, 1)] + [(0, 1)]
+    steps = [(k, flip) for flip in (1, 0) for k in (2, 1, 3)] + [(0, 1)]
     x_peers = [(me, lax.rem(x + k, SIDE)) for k in (1, 2, 3)]
     y_peers = [(device(dy=k, flip=f), x) for k, f in steps]
     z_peers = [(device(dz=k, flip=f), x) for k, f in steps]

time: 64.8 us -> 64.8 us (level)
  no operation moved by 1% of the time
where the time goes in v8:
time: 64.8 us; the launch traced here: 64.6 us
  Pallas kernels  64 us (99%)
    pallas_call x1, Pallas kernels, body(): pl.pallas_call(kernel, out_shape=(pltpu.VMEM((total, columns), bf16), plt...  57.8 us
    pallas_call x1, Pallas kernels, body(): pl.pallas_call(deliver, out_shape=(jax.ShapeDtypeStruct((total, columns),...  6.2 us

profile of v8, /device:TPU:1, one launch (start us, length us, event | category | flops | bytes accessed | tf_op | source)
XLA Modules:
  0.0 64.6 jit_solution(8080148326175945338)
XLA Ops:
  0.6 57.8 %shard_map.135 = (bf16[2048,2048]{1,0:T(8,128)(2,1)S(1)}, bf16[2048,2048]{1,0:T(8,128)(2,1)S(1)}, f32[2,64,2048]{2,1,0:T(8,128)S(1)}, f32[2,1,4096]{2,1,0:T(1,128)S(1)}) custom-call(f32[64,2048]{1,0:T(8,128)} %wg.1, f32[64,2048]{1,0:T(8,128)} %mg.1, f32[64,2048]{1,0:T(8,128)} %sg.1, f32[64,2048]{1,0:T(8,128)} %wu.1, f32[64,2048]{1,0:T(8,128)} %mu.1, ...), custom_call_target="tpu_custom_call" | custom-call | tf_op jit(solution)/shard_map/pallas_call | solution.py:443
  58.4 6.2 %shard_map.136 = (bf16[2048,2048]{1,0:T(8,128)(2,1)}, bf16[2048,2048]{1,0:T(8,128)(2,1)}, f32[1,2048]{1,0:T(1,128)}, f32[1,2048]{1,0:T(1,128)}, bf16[2048]{0:T(1...) custom-call(bf16[2048,2048]{1,0:T(8,128)(2,1)S(1)} %get-tuple-element.18.big_g, ...), custom_call_target="tpu_custom_call" | custom-call | tf_op jit(solution)/shard_map/pallas_call | solution.py:479
